TPU v7x, 128 devices: a whole 4x4x4 slice. The times are simulated.
128 devices in a mesh: row: 16 (over z, y), col: 8 (over x, core).
Axes of the slice: x: 4, y: 4, z: 4, core: 2. Of those that a mesh axis runs over, the one named last changes fastest.
Arguments:
- pair: bfloat16 [768, 768, 128], P('row', 'col'), may hold values from -6 to 6
- chain_lengths: int32 [8], replicated, may hold values from 1 to 96, 576 in all
- gains: float32 [2, 2, 128], replicated, may hold values from 0.1 to 1.9
- biases: float32 [2, 2, 128], replicated, may hold values from -3 to 3
- w_in: bfloat16 [2, 128, 640], replicated, may hold values from -0.5 to 0.5
- w_out: bfloat16 [2, 128, 128], replicated, may hold values from -0.5 to 0.5
Outputs:
- pair_out: bfloat16 [768, 768, 128], P('row', 'col')
Inputs may be any that keep to these rules, and one draw needn't show every extreme that they name: Chain k occupies positions k * 96 to (k + 1) * 96 - 1 and its live residues are the first chain_lengths[k] of them; the lengths sum to 576 and one of them equals 96.
All inputs are finite; a program needn't handle non-finite values.
Results may differ from a plain program's by a relative error of at most 0.0054.
Values may be sent and summed in bfloat16 or wider, within the bound.
No kernel may reach another device: no remote copies, remote signals or barrier semaphores. Data moves between devices by JAX's collectives and lax.ppermute only.
A program may use at most 64 MiB of HBM per device.

v0:
```python
import jax
import jax.numpy as jnp
from jax import lax
from jax.sharding import PartitionSpec as P

N = 768
NCHAIN = 8


def cut_along(value, dim, count):
    lengths = value.shape
    blocks = value.reshape(*lengths[:dim], count, lengths[dim] // count, *lengths[dim + 1 :])
    return jnp.moveaxis(blocks, dim, 0)


def joined_along(blocks, dim):
    blocks = jnp.moveaxis(blocks, 0, dim)
    lengths = blocks.shape
    return blocks.reshape(*lengths[:dim], lengths[dim] * lengths[dim + 1], *lengths[dim + 2 :])


def exchange_both(value, axis, axes, splits, concats):
    sizes = [lax.axis_size(a) for a in axes]
    blocks = cut_along(value, splits[0], sizes[0])
    blocks = jnp.moveaxis(cut_along(blocks, splits[1] + 1, sizes[1]), 0, 1)
    inside = blocks.shape[2:]
    blocks = blocks.reshape(-1, *inside)
    blocks = lax.all_to_all(blocks, axis, split_axis=0, concat_axis=0, tiled=True)
    blocks = joined_along(blocks.reshape(*sizes, *inside), concats[0] + 1)
    return joined_along(blocks, concats[1])


def layer_norm(values, gain_vec, bias_vec, axis_pos):
    wide = values.astype(jnp.float32)
    average = jnp.mean(wide, axis=axis_pos, keepdims=True)
    centred = wide - average
    variance = jnp.mean(centred * centred, axis=axis_pos, keepdims=True)
    return centred * jax.lax.rsqrt(variance + 1e-05) * gain_vec + bias_vec


def live_values(global_index, chain_lengths):
    slot_size = N // NCHAIN
    chain_index = global_index // slot_size
    offset = global_index % slot_size
    matches = chain_index[:, None] == jnp.arange(NCHAIN, dtype=jnp.int32)[None, :]
    live_length = jnp.sum(jnp.where(matches, chain_lengths[None, :], 0), axis=1)
    return (offset < live_length).astype(jnp.float32)


def regroup(values_in, n_row, n_col, owned_count):
    grouped = values_in.reshape((n_row, n_col, owned_count) + values_in.shape[1:])
    return jnp.swapaxes(grouped, 0, 1).reshape(values_in.shape)


def body(pair, chain_lengths, gains, biases, w_in, w_out):
    tile_rows, tile_cols, channels = pair.shape
    n_row = lax.axis_size("row")
    n_col = lax.axis_size("col")
    owned_count = channels // (n_row * n_col)
    row_index = lax.axis_index("row") * tile_rows + jnp.arange(tile_rows, dtype=jnp.int32)
    col_index = lax.axis_index("col") * tile_cols + jnp.arange(tile_cols, dtype=jnp.int32)
    pmask = (
        live_values(row_index, chain_lengths)[:, None]
        * live_values(col_index, chain_lengths)[None, :]
    )

    def return_products(products):
        return exchange_both(products, ("row", "col"), ("row", "col"), (1, 2), (0, 0))

    state = pair
    for update_index in range(2):
        weights_in = w_in[update_index]
        normed = layer_norm(state, gains[update_index, 0], biases[update_index, 0], 2).astype(
            jnp.bfloat16
        )

        def project_first(column_block):
            block = weights_in[:, column_block * channels : (column_block + 1) * channels]
            return jnp.einsum("ijc,cd->dij", normed, block, preferred_element_type=jnp.float32)

        left_edges = (pmask[None] * jax.nn.sigmoid(project_first(1)) * project_first(0)).astype(
            jnp.bfloat16
        )
        right_edges = (pmask[None] * jax.nn.sigmoid(project_first(3)) * project_first(2)).astype(
            jnp.bfloat16
        )
        left_full = exchange_both(left_edges, ("row", "col"), ("row", "col"), (0, 0), (1, 2))
        right_full = exchange_both(right_edges, ("row", "col"), ("row", "col"), (0, 0), (1, 2))
        if update_index == 1:
            products = jnp.einsum(
                "cki,ckj->cij", left_full, right_full, preferred_element_type=jnp.float32
            )
        else:
            products = jnp.einsum(
                "cik,cjk->cij", left_full, right_full, preferred_element_type=jnp.float32
            )
        returned = return_products(products.astype(jnp.bfloat16))
        gain_out = gains[update_index, 1]
        bias_out = biases[update_index, 1]
        weights_out = w_out[update_index]
        gain_out = regroup(gain_out, n_row, n_col, owned_count)
        bias_out = regroup(bias_out, n_row, n_col, owned_count)
        weights_out = regroup(weights_out, n_row, n_col, owned_count)
        normed_out = layer_norm(
            returned, gain_out[:, None, None], bias_out[:, None, None], 0
        ).astype(jnp.bfloat16)
        mixed = jnp.einsum(
            "cij,cd->ijd", normed_out, weights_out, preferred_element_type=jnp.float32
        )
        gate_vals = jax.nn.sigmoid(
            jnp.dot(
                normed.reshape(tile_rows * tile_cols, channels),
                weights_in[:, 4 * channels : 5 * channels],
                preferred_element_type=jnp.float32,
            ).reshape(tile_rows, tile_cols, channels)
        )
        state = (state.astype(jnp.float32) + gate_vals * mixed).astype(jnp.bfloat16)
    return state


def solution(mesh):
    placed = (P("row", "col", None), P(), P(), P(), P(), P())
    return jax.shard_map(
        body, mesh=mesh, in_specs=placed, out_specs=P("row", "col", None), check_vma=False
    )
```

profile of v0, /device:TPU:1, one launch (start us, length us, event | category | flops | bytes accessed | tf_op | source)
XLA Modules:
  0.0 234.6 jit_solution(11512404190657771769)
XLA Ops:
  1.7 1.8 convert_reduce_fusion.1
  3.5 2.7 %fusion.24 = f32[48,96]{1,0:T(8,128)S(1)} fusion(bf16[48,96,128]{2,1,0:T(8,128)(2,1)} %param.6, f32[48,96]{1,0:T(8,128)S(1)} %broadcast_multiply_fusion.4), kind=kLoop, calls=%fused_computation.32 | loop fusion | flops 2354688 | bytes 1216512 | tf_op jit(solution)/shard_map/reduce_sum | solution.py:37
  7.7 2.4 %fusion.35 = bf16[128,1,48,96]{0,3,2,1:T(8,128)(2,1)S(1)} fusion(f32[48,96,128]{2,1,0:T(8,128)S(1)} %fusion.43, f32[48,96]{1,0:T(8,128)S(1)} %get-tuple-element.26, bf16[128,640]{1,0:T(8,128)(2,1)S(1)} %get-tuple-element.10, bf16[48,96,128]{2,1,0:T(8,128)(2,1)S(1)} %copy-done, f32[128]{0:T(128)S(1)} %get-tuple-element.16, f32[128]{0:T(128)S(1)} %get-tuple-element.23, ...), kind=kOutput, calls=%fused_computation.51 | convolution fusion | flops 158072832 | bytes 4826112 | tf_op jit(solution)/shard_map/ijc,cd->dij/dot_general | solution.py:79
  10.1 1.8 copy.70
  11.9 11.5 %all-to-all-start.1 = ((bf16[128,1,48,96]{3,2,1,0:T(8,128)(2,1)}), bf16[128,1,48,96]{3,2,1,0:T(8,128)(2,1)S(1)}, u32[]{:S(2)}, u32[]{:S(2)}) async-start(bf16[128,1,48,96]{3,2,1,0:T(8,128)(2,1)} %copy.70), calls=%async_computation.1 | async-start | bytes 3145728 | tf_op jit(solution)/shard_map/all_to_all | solution.py:28
  24.8 3.6 %fusion.34 = bf16[128,1,48,96]{0,3,2,1:T(8,128)(2,1)} fusion(f32[48,96,128]{2,1,0:T(8,128)S(1)} %fusion.44, f32[48,96]{1,0:T(8,128)S(1)} %get-tuple-element.26, bf16[128,640]{1,0:T(8,128)(2,1)S(1)} %get-tuple-element.10, bf16[48,96,128]{2,1,0:T(8,128)(2,1)S(1)} %copy-done, f32[128]{0:T(128)S(1)} %get-tuple-element.16, f32[128]{0:T(128)S(1)} %get-tuple-element.23, ...), kind=kOutput, calls=%fused_computation.50 | convolution fusion | flops 158072832 | bytes 4826112 | tf_op jit(solution)/shard_map/ijc,cd->dij/dot_general | solution.py:79
  28.5 2.8 %copy.67 = bf16[128,1,48,96]{3,2,1,0:T(8,128)(2,1)} copy(bf16[128,1,48,96]{0,3,2,1:T(8,128)(2,1)} %fusion.34) | data formatting | bytes 2359296 | tf_op jit(solution)/shard_map/reshape;reshape;reshape | solution.py:27
  31.3 17.0 %all-to-all-done.1 = bf16[128,1,48,96]{3,2,1,0:T(8,128)(2,1)S(1)} async-done(((bf16[128,1,48,96]{3,2,1,0:T(8,128)(2,1)}), bf16[128,1,48,96]{3,2,1,0:T(8,128)(2,1)S(1)}, u32[]{:S(2)}, u32[]{:S(2)}) %all-to-all-start.1) | async-done | bytes 1179680 | tf_op jit(solution)/shard_map/all_to_all | solution.py:28
  48.3 5.4 %all-to-all-start = ((bf16[128,1,48,96]{3,2,1,0:T(8,128)(2,1)}), bf16[128,1,48,96]{3,2,1,0:T(8,128)(2,1)}, u32[]{:S(2)}, u32[]{:S(2)}) async-start(bf16[128,1,48,96]{3,2,1,0:T(8,128)(2,1)} %copy.67), calls=%async_computation | async-start | bytes 3145728 | tf_op jit(solution)/shard_map/all_to_all | solution.py:28
  54.9 2.5 %copy.72 = bf16[8,1,768,96]{2,3,0,1:T(8,128)(2,1)} copy(bf16[8,1,768,96]{3,2,0,1:T(8,128)(2,1)} %bitcast.208) | data formatting | bytes 2359296 | tf_op jit(solution)/shard_map/reshape | solution.py:19
  57.4 20.9 %all-to-all-done = bf16[128,1,48,96]{3,2,1,0:T(8,128)(2,1)} async-done(((bf16[128,1,48,96]{3,2,1,0:T(8,128)(2,1)}), bf16[128,1,48,96]{3,2,1,0:T(8,128)(2,1)}, u32[]{:S(2)}, u32[]{:S(2)}) %all-to-all-start) | async-done | bytes 1179680 | tf_op jit(solution)/shard_map/all_to_all | solution.py:28
  81.4 3.8 %bitcast_convert_fusion = bf16[768,768]{1,0:T(8,128)(2,1)} fusion(bf16[8,1,768,96]{2,3,0,1:T(8,128)(2,1)} %copy.72, bf16[8,1,768,96]{2,3,0,1:T(8,128)(2,1)} %copy.69), kind=kOutput, calls=%fused_computation.40 | convolution fusion | flops 906559488 | bytes 3538944 | tf_op jit(solution)/shard_map/cik,cjk->cij/dot_general | solution.py:94
  85.2 3.1 %reshape_transpose_reshape.6 = bf16[16,1,48,8,96]{4,3,2,0,1:T(8,128)(2,1)S(1)} reshape(bf16[768,768]{1,0:T(8,128)(2,1)} %bitcast_convert_fusion) | data formatting | bytes 2359296 | tf_op jit(solution)/shard_map/reshape;transpose;reshape | solution.py:12
  89.8 4.4 %all-to-all-start.2 = ((bf16[128,1,48,96]{3,2,1,0:T(8,128)(2,1)}), bf16[128,1,48,96]{3,2,1,0:T(8,128)(2,1)S(1)}, u32[]{:S(2)}, u32[]{:S(2)}) async-start(bf16[128,1,48,96]{3,2,1,0:T(8,128)(2,1)} %bitcast.207), calls=%async_computation.2 | async-start | bytes 3145728 | tf_op jit(solution)/shard_map/all_to_all | solution.py:28
  94.3 3.4 %fusion.45 = f32[48,96,128]{2,1,0:T(8,128)} fusion(bf16[128,640]{1,0:T(8,128)(2,1)S(1)} %get-tuple-element.10, bf16[48,96,128]{2,1,0:T(8,128)(2,1)S(1)} %copy-done, f32[128]{0:T(128)S(1)} %get-tuple-element.16, f32[128]{0:T(128)S(1)} %get-tuple-element.23, f32[48,96]{1,0:T(8,128)S(1)} %get-tuple-element.25, f32[48,96]{1,0:T(8,128)S(1)} %broadcast_multiply_fusion.4), kind=kOutput, calls=%fused_computation.73 | convolution fusion | flops 154533888 | bytes 3621888 | tf_op jit(solution)/shard_map/dot_general | solution.py:111
  97.7 21.4 %all-to-all-done.2 = bf16[128,1,48,96]{3,2,1,0:T(8,128)(2,1)S(1)} async-done(((bf16[128,1,48,96]{3,2,1,0:T(8,128)(2,1)}), bf16[128,1,48,96]{3,2,1,0:T(8,128)(2,1)S(1)}, u32[]{:S(2)}, u32[]{:S(2)}) %all-to-all-start.2) | async-done | bytes 1179680 | tf_op jit(solution)/shard_map/all_to_all | solution.py:28
  121.2 1.7 convert_reduce_fusion
  126.0 2.4 %fusion.36 = bf16[128,1,48,96]{0,3,2,1:T(8,128)(2,1)S(1)} fusion(f32[48,96,128]{2,1,0:T(8,128)S(1)} %fusion.41, f32[48,96]{1,0:T(8,128)S(1)} %get-tuple-element.26, bf16[128,640]{1,0:T(8,128)(2,1)S(1)} %get-tuple-element.9, bf16[48,96,128]{2,1,0:T(8,128)(2,1)S(1)} %get-tuple-element.20, f32[128]{0:T(128)S(1)} %get-tuple-element.15, ...), kind=kOutput, calls=%fused_computation.52 | convolution fusion | flops 158072832 | bytes 4826112 | tf_op jit(solution)/shard_map/ijc,cd->dij/dot_general | solution.py:79
  128.4 1.8 copy.81
  130.2 4.4 %all-to-all-start.3 = ((bf16[128,1,48,96]{3,2,1,0:T(8,128)(2,1)}), bf16[128,1,48,96]{3,2,1,0:T(8,128)(2,1)S(1)}, u32[]{:S(2)}, u32[]{:S(2)}) async-start(bf16[128,1,48,96]{3,2,1,0:T(8,128)(2,1)} %copy.81), calls=%async_computation.3 | async-start | bytes 3145728 | tf_op jit(solution)/shard_map/all_to_all | solution.py:28
  136.0 3.6 %fusion.37 = bf16[128,1,48,96]{0,3,2,1:T(8,128)(2,1)} fusion(f32[48,96,128]{2,1,0:T(8,128)S(1)} %fusion.40, f32[48,96]{1,0:T(8,128)S(1)} %get-tuple-element.26, bf16[128,640]{1,0:T(8,128)(2,1)S(1)} %get-tuple-element.9, bf16[48,96,128]{2,1,0:T(8,128)(2,1)S(1)} %get-tuple-element.20, f32[128]{0:T(128)S(1)} %get-tuple-element.15, ...), kind=kOutput, calls=%fused_computation.53 | convolution fusion | flops 158072832 | bytes 4826112 | tf_op jit(solution)/shard_map/ijc,cd->dij/dot_general | solution.py:79
  139.6 2.8 %copy.84 = bf16[128,1,48,96]{3,2,1,0:T(8,128)(2,1)} copy(bf16[128,1,48,96]{0,3,2,1:T(8,128)(2,1)} %fusion.37) | data formatting | bytes 2359296 | tf_op jit(solution)/shard_map/reshape;reshape;reshape | solution.py:27
  142.4 17.2 %all-to-all-done.3 = bf16[128,1,48,96]{3,2,1,0:T(8,128)(2,1)S(1)} async-done(((bf16[128,1,48,96]{3,2,1,0:T(8,128)(2,1)}), bf16[128,1,48,96]{3,2,1,0:T(8,128)(2,1)S(1)}, u32[]{:S(2)}, u32[]{:S(2)}) %all-to-all-start.3) | async-done | bytes 1179680 | tf_op jit(solution)/shard_map/all_to_all | solution.py:28
  159.6 5.4 %all-to-all-start.4 = ((bf16[128,1,48,96]{3,2,1,0:T(8,128)(2,1)}), bf16[128,1,48,96]{3,2,1,0:T(8,128)(2,1)}, u32[]{:S(2)}, u32[]{:S(2)}) async-start(bf16[128,1,48,96]{3,2,1,0:T(8,128)(2,1)} %copy.84), calls=%async_computation.4 | async-start | bytes 3145728 | tf_op jit(solution)/shard_map/all_to_all | solution.py:28
  166.2 2.5 %copy.83 = bf16[1,768,8,96]{1,3,2,0:T(8,128)(2,1)} copy(bf16[1,768,8,96]{3,1,2,0:T(8,128)(2,1)} %bitcast.210) | data formatting | bytes 2359296 | tf_op jit(solution)/shard_map/transpose | solution.py:17
  168.7 20.9 %all-to-all-done.4 = bf16[128,1,48,96]{3,2,1,0:T(8,128)(2,1)} async-done(((bf16[128,1,48,96]{3,2,1,0:T(8,128)(2,1)}), bf16[128,1,48,96]{3,2,1,0:T(8,128)(2,1)}, u32[]{:S(2)}, u32[]{:S(2)}) %all-to-all-start.4) | async-done | bytes 1179680 | tf_op jit(solution)/shard_map/all_to_all | solution.py:28
  192.6 3.8 %convolution_convert_fusion = bf16[768,768]{1,0:T(8,128)(2,1)} fusion(bf16[768,768]{0,1:T(8,128)(2,1)} %bitcast.212, bf16[768,768]{0,1:T(8,128)(2,1)} %bitcast.213), kind=kOutput, calls=%fused_computation.49 | convolution fusion | flops 906559488 | bytes 3538944 | tf_op jit(solution)/shard_map/cki,ckj->cij/dot_general | solution.py:90
  196.4 3.1 %reshape_transpose_reshape.7 = bf16[16,1,48,8,96]{4,3,2,0,1:T(8,128)(2,1)S(1)} reshape(bf16[768,768]{1,0:T(8,128)(2,1)} %convolution_convert_fusion) | data formatting | bytes 2359296 | tf_op jit(solution)/shard_map/reshape;transpose;reshape | solution.py:12
  201.0 4.4 %all-to-all-start.5 = ((bf16[128,1,48,96]{3,2,1,0:T(8,128)(2,1)}), bf16[128,1,48,96]{3,2,1,0:T(8,128)(2,1)S(1)}, u32[]{:S(2)}, u32[]{:S(2)}) async-start(bf16[128,1,48,96]{3,2,1,0:T(8,128)(2,1)} %bitcast.206), calls=%async_computation.5 | async-start | bytes 3145728 | tf_op jit(solution)/shard_map/all_to_all | solution.py:28
  205.6 3.4 %fusion.42 = f32[48,96,128]{2,1,0:T(8,128)} fusion(bf16[128,640]{1,0:T(8,128)(2,1)S(1)} %get-tuple-element.9, bf16[48,96,128]{2,1,0:T(8,128)(2,1)S(1)} %get-tuple-element.20, f32[128]{0:T(128)S(1)} %get-tuple-element.15, f32[128]{0:T(128)S(1)} %get-tuple-element.24, f32[48,96]{1,0:T(8,128)S(1)} %add_rsqrt_fusion.1, f32[48,96]{1,0:T(8,128)S(1)} %broadcast_multiply_fusion.2), kind=kOutput, calls=%fused_computation.65 | convolution fusion | flops 154533888 | bytes 3621888 | tf_op jit(solution)/shard_map/dot_general | solution.py:111
  209.0 21.5 %all-to-all-done.5 = bf16[128,1,48,96]{3,2,1,0:T(8,128)(2,1)S(1)} async-done(((bf16[128,1,48,96]{3,2,1,0:T(8,128)(2,1)}), bf16[128,1,48,96]{3,2,1,0:T(8,128)(2,1)S(1)}, u32[]{:S(2)}, u32[]{:S(2)}) %all-to-all-start.5) | async-done | bytes 1179680 | tf_op jit(solution)/shard_map/all_to_all | solution.py:28
  232.4 2.1 fusion.29
  (53 shorter events, 24.9 us)
Async XLA Ops:
  0.0 6.3 %copy-start = (bf16[48,96,128]{2,1,0:T(8,128)(2,1)S(1)}, bf16[48,96,128]{2,1,0:T(8,128)(2,1)}, u32[]{:S(2)}) copy-start(bf16[48,96,128]{2,1,0:T(8,128)(2,1)} %param.6) | copy-start | bytes 3538948
  0.0 6.2 %copy-start.3 = (bf16[2,128,640]{2,1,0:T(8,128)(2,1)S(1)}, bf16[2,128,640]{2,1,0:T(8,128)(2,1)}, u32[]{:S(2)}) copy-start(bf16[2,128,640]{2,1,0:T(8,128)(2,1)} %param.10) | copy-start | bytes 983044
  0.0 6.2 %copy-start.4 = (f32[2,2,128]{2,1,0:T(2,128)S(1)}, f32[2,2,128]{2,1,0:T(2,128)}, u32[]{:S(2)}) copy-start(f32[2,2,128]{2,1,0:T(2,128)} %param.9) | copy-start | bytes 6148
  0.0 6.2 %copy-start.5 = (f32[2,2,128]{2,1,0:T(2,128)S(1)}, f32[2,2,128]{2,1,0:T(2,128)}, u32[]{:S(2)}) copy-start(f32[2,2,128]{2,1,0:T(2,128)} %param.8) | copy-start | bytes 6148
  11.9 36.3 %all-to-all-start.1 = ((bf16[128,1,48,96]{3,2,1,0:T(8,128)(2,1)}), bf16[128,1,48,96]{3,2,1,0:T(8,128)(2,1)S(1)}, u32[]{:S(2)}, u32[]{:S(2)}) async-start(bf16[128,1,48,96]{3,2,1,0:T(8,128)(2,1)} %copy.70), calls=%async_computation.1 | async-start | bytes 3145728 | tf_op jit(solution)/shard_map/all_to_all | solution.py:28
  48.3 30.1 %all-to-all-start = ((bf16[128,1,48,96]{3,2,1,0:T(8,128)(2,1)}), bf16[128,1,48,96]{3,2,1,0:T(8,128)(2,1)}, u32[]{:S(2)}, u32[]{:S(2)}) async-start(bf16[128,1,48,96]{3,2,1,0:T(8,128)(2,1)} %copy.67), calls=%async_computation | async-start | bytes 3145728 | tf_op jit(solution)/shard_map/all_to_all | solution.py:28
  89.8 29.4 %all-to-all-start.2 = ((bf16[128,1,48,96]{3,2,1,0:T(8,128)(2,1)}), bf16[128,1,48,96]{3,2,1,0:T(8,128)(2,1)S(1)}, u32[]{:S(2)}, u32[]{:S(2)}) async-start(bf16[128,1,48,96]{3,2,1,0:T(8,128)(2,1)} %bitcast.207), calls=%async_computation.2 | async-start | bytes 3145728 | tf_op jit(solution)/shard_map/all_to_all | solution.py:28
  119.5 1.7 copy-start.1
  119.5 1.7 copy-start.6
  130.2 29.4 %all-to-all-start.3 = ((bf16[128,1,48,96]{3,2,1,0:T(8,128)(2,1)}), bf16[128,1,48,96]{3,2,1,0:T(8,128)(2,1)S(1)}, u32[]{:S(2)}, u32[]{:S(2)}) async-start(bf16[128,1,48,96]{3,2,1,0:T(8,128)(2,1)} %copy.81), calls=%async_computation.3 | async-start | bytes 3145728 | tf_op jit(solution)/shard_map/all_to_all | solution.py:28
  159.6 30.1 %all-to-all-start.4 = ((bf16[128,1,48,96]{3,2,1,0:T(8,128)(2,1)}), bf16[128,1,48,96]{3,2,1,0:T(8,128)(2,1)}, u32[]{:S(2)}, u32[]{:S(2)}) async-start(bf16[128,1,48,96]{3,2,1,0:T(8,128)(2,1)} %copy.84), calls=%async_computation.4 | async-start | bytes 3145728 | tf_op jit(solution)/shard_map/all_to_all | solution.py:28
  201.0 29.4 %all-to-all-start.5 = ((bf16[128,1,48,96]{3,2,1,0:T(8,128)(2,1)}), bf16[128,1,48,96]{3,2,1,0:T(8,128)(2,1)S(1)}, u32[]{:S(2)}, u32[]{:S(2)}) async-start(bf16[128,1,48,96]{3,2,1,0:T(8,128)(2,1)} %bitcast.206), calls=%async_computation.5 | async-start | bytes 3145728 | tf_op jit(solution)/shard_map/all_to_all | solution.py:28
  230.8 1.7 copy-start.2
where the time goes:
time: 236 us; the launch traced here: 235 us
  waiting for transfers between devices  119 us (50%)
  matrix products  35.8 us (15%)
  starting transfers between devices  35.5 us (15%)
  local copies, waits for them, and re-layouts  33.1 us (14%)
  other arithmetic  11 us (5%)
    all_to_all x6, waiting for transfers between devices, exchange_both(): lax.all_to_all(blocks, axis, split_axis=0, concat_axis=0, tiled=True)  119 us
    all_to_all x6, starting transfers between devices, exchange_both(): lax.all_to_all(blocks, axis, split_axis=0, concat_axis=0, tiled=True)  35.5 us
    dot_general x8, matrix products, project_first(): jnp.einsum('ijc,cd->dij', normed, block, preferred_element_type=jnp.float32)  17.7 us
    transpose x6, local copies, waits for them, and re-layouts, joined_along(): blocks = jnp.moveaxis(blocks, 0, dim)  9.49 us
    another operation x4, local copies, waits for them, and re-layouts, exchange_both(): blocks = blocks.reshape(-1, *inside)  9.18 us
    another operation x4, local copies, waits for them, and re-layouts, cut_along(): value.reshape(*lengths[:dim], count, lengths[dim] // count, *lengths[dim...  9.16 us
    dot_general x2, matrix products, body(): jnp.dot(normed.reshape(tile_rows * tile_cols, channels), weights_in[:, 4...  6.74 us
    reduce_sum x4, other arithmetic, layer_norm(): variance = jnp.mean(centred * centred, axis=axis_pos, keepdims=True)  5.44 us
  transfers between devices with their start and end apart: 6, of which 6 were waited for; matrix products, arithmetic and copies ran while one was open for 13% of the time, Pallas kernels for 0%

commit v1 on v0

v1 whole, which is shorter than its diff:
```python
import functools
import jax
import jax.numpy as jnp
from jax import lax
from jax.experimental import pallas as pl
from jax.experimental.pallas import tpu as pltpu
from jax.sharding import PartitionSpec as P

N = 768
NCHAIN = 8
C = 128
ROWS, COLS = 16, 8
TR, TC = N // ROWS, N // COLS
ILO, IHI, KHI, KLO = 4, 12, 3, 32
NQ = IHI * KHI
SA = 2 * NQ
SP = 40
BF, F32 = jnp.bfloat16, jnp.float32


def live_values(global_index, chain_lengths):
    slot_size = N // NCHAIN
    chain_index = global_index // slot_size
    offset = global_index % slot_size
    matches = chain_index[:, None] == jnp.arange(NCHAIN, dtype=jnp.int32)[None, :]
    live_length = jnp.sum(jnp.where(matches, chain_lengths[None, :], 0), axis=1)
    return (offset < live_length).astype(F32)


def sigmoid(x):
    return 0.5 * jnp.tanh(0.5 * x) + 0.5


def norm_rows(z, gain, bias):
    wide = z.astype(F32)
    mean = jnp.mean(wide, axis=1, keepdims=True)
    centred = wide - mean
    var = jnp.mean(centred * centred, axis=1, keepdims=True)
    return centred * lax.rsqrt(var + 1e-05) * gain + bias


def pre_kernel(z_ref, w_ref, gb_ref, mask_ref, out_ref, scr):
    gain = gb_ref[0:1, :]
    bias = gb_ref[1:2, :]

    def step(t, carry):
        for h in range(KHI):
            parts = []
            for e in range(2):
                z = z_ref[:, 2 * t + e, h * KLO:(h + 1) * KLO, :].reshape(C, C)
                parts.append(norm_rows(z, gain, bias).astype(BF))
            normed = jnp.concatenate(parts, axis=0)
            rows = [h * IHI + 2 * t + e for e in range(2)]
            mask = jnp.concatenate([mask_ref[pl.ds(r, 1), :] for r in rows], axis=1)
            for side in range(2):
                value, gate = (
                    lax.dot_general(
                        w_ref[(2 * side + k) * C:(2 * side + k + 1) * C, :], normed,
                        (((1,), (1,)), ((), ())), preferred_element_type=F32)
                    for k in range(2)
                )
                edges = mask * sigmoid(gate) * value
                for e in range(2):
                    row = h * 2 * IHI + side * IHI + 2 * t + e
                    scr[pl.ds(row, C, stride=SA), :] = edges[:, e * C:(e + 1) * C]
        return carry

    lax.fori_loop(0, IHI // 2, step, 0)

    def cast(s, carry):
        out_ref[s] = scr[pl.ds(pl.multiple_of(s * SA, 8), 2 * NQ), :].astype(BF)
        return carry

    lax.fori_loop(0, C, cast, 0, unroll=4)


def swap_blocks(x):
    lane = lax.broadcasted_iota(jnp.int32, x[0].shape, 1)
    low64 = lane < 64
    low32 = (lane % 64) < 32
    t = [None] * 4
    for b in range(2):
        t[b] = jnp.where(low64, x[b], pltpu.roll(x[b + 2], 64, 1))
        t[b + 2] = jnp.where(low64, pltpu.roll(x[b], 64, 1), x[b + 2])
    y = []
    for b in (0, 2):
        y.append(jnp.where(low32, t[b], pltpu.roll(t[b + 1], 32, 1)))
        y.append(jnp.where(low32, pltpu.roll(t[b], 96, 1), t[b + 1]))
    return y


def tri_kernel(in_ref, out_ref, ml, mr, mlb, mrb, tri, oscr, *, incoming):
    def gather(r, carry):
        for v in range(6):
            x = []
            for b in range(4):
                c, h = divmod(4 * v + b, KHI)
                whole = in_ref[r * COLS + c].astype(F32)
                x.append(whole[h * 24:(h + 1) * 24, :])
            y = swap_blocks(x)
            for a in range(4):
                rows, lanes = slice(a * IHI, (a + 1) * IHI), slice(v * C, (v + 1) * C)
                ml[r, rows, lanes] = y[a][0:IHI]
                mr[r, rows, lanes] = y[a][IHI:2 * IHI]
        return carry

    lax.fori_loop(0, ROWS, gather, 0)
    mlb[...] = ml[...].reshape(N, N).astype(BF)
    mrb[...] = mr[...].reshape(N, N).astype(BF)
    for m in range(2):
        cut = slice(m * 384, (m + 1) * 384)
        if incoming:
            block = lax.dot_general(
                mlb[:, cut], mrb[...], (((0,), (0,)), ((), ())), preferred_element_type=F32)
        else:
            block = lax.dot_general(
                mlb[cut, :], mrb[...], (((1,), (1,)), ((), ())), preferred_element_type=F32)
        tri[m * 8:(m + 1) * 8] = block.reshape(8, TR, N)

    def scatter(r, carry):
        for v in range(6):
            x = [tri[r, a * IHI:(a + 1) * IHI, v * C:(v + 1) * C] for a in range(4)]
            y = swap_blocks(x)
            for b in range(4):
                c, h = divmod(4 * v + b, KHI)
                oscr[r * COLS + c, h * IHI:(h + 1) * IHI, :] = y[b]
        return carry

    lax.fori_loop(0, ROWS, scatter, 0)

    def cast(s, carry):
        out_ref[s] = oscr[s].astype(BF)
        return carry

    lax.fori_loop(0, C, cast, 0, unroll=4)


def post_kernel(in_ref, z_ref, gate_ref, gb_ref, w_ref, out_ref, scr):
    gain = jnp.broadcast_to(gb_ref[:, 0:1], (C, C))
    bias = jnp.broadcast_to(gb_ref[:, 1:2], (C, C))

    def widen(s, carry):
        scr[pl.ds(pl.multiple_of(s * SP, 8), NQ), :] = in_ref[s].astype(F32)
        return carry

    lax.fori_loop(0, C, widen, 0, unroll=4)

    def step(t, carry):
        for h in range(KHI):
            x = scr[pl.ds(h * IHI + t, C, stride=SP), :]
            mean = jnp.mean(x, axis=0, keepdims=True)
            centred = x - mean
            var = jnp.mean(centred * centred, axis=0, keepdims=True)
            normed = (centred * lax.rsqrt(var + 1e-05) * gain + bias).astype(BF)
            mixed = lax.dot_general(
                normed, w_ref[...], (((0,), (0,)), ((), ())), preferred_element_type=F32)
            cut = slice(h * KLO, (h + 1) * KLO)
            z = z_ref[:, t, cut, :].reshape(C, C).astype(F32)
            gate = gate_ref[:, t, cut, :].reshape(C, C)
            out_ref[:, t, cut, :] = (z + gate * mixed).astype(BF).reshape(ILO, KLO, C)
        return carry

    lax.fori_loop(0, IHI, step, 0)


def body(pair, chain_lengths, gains, biases, w_in, w_out):
    axes = ("row", "col")
    row_live = live_values(lax.axis_index("row") * TR + jnp.arange(TR, dtype=jnp.int32), chain_lengths)
    col_live = live_values(lax.axis_index("col") * TC + jnp.arange(TC, dtype=jnp.int32), chain_lengths)
    mask = (
        row_live.reshape(ILO, IHI).T[None, :, :, None] * col_live.reshape(KHI, 1, 1, KLO)
    ).reshape(NQ, C)
    state = pair.reshape(ILO, IHI, TC, C)
    for u in range(2):
        w = w_in[u]
        w_t = w[:, :4 * C].T
        gb_in = jnp.stack([gains[u, 0], biases[u, 0]])
        factors = pl.pallas_call(
            pre_kernel,
            out_shape=jax.ShapeDtypeStruct((C, 2 * NQ, C), BF),
            scratch_shapes=[pltpu.VMEM((C * SA, C), F32)],
            name="pre",
        )(state, w_t, gb_in, mask)
        factors = lax.all_to_all(factors, axes, 0, 0, tiled=True)
        normed = norm_rows(state.reshape(-1, C), gains[u, 0], biases[u, 0]).astype(BF)
        gate = jax.nn.sigmoid(jnp.dot(normed, w[:, 4 * C:], preferred_element_type=F32))
        gate = gate.reshape(ILO, IHI, TC, C)
        products = pl.pallas_call(
            functools.partial(tri_kernel, incoming=u == 1),
            out_shape=jax.ShapeDtypeStruct((C, NQ, C), BF),
            scratch_shapes=[
                pltpu.VMEM((ROWS, TR, N), F32), pltpu.VMEM((ROWS, TR, N), F32),
                pltpu.VMEM((N, N), BF), pltpu.VMEM((N, N), BF),
                pltpu.VMEM((ROWS, TR, N), F32), pltpu.VMEM((C, NQ, C), F32),
            ],
            name="tri",
        )(factors)
        products = lax.all_to_all(products, axes, 0, 0, tiled=True)
        gb_out = jnp.stack([gains[u, 1], biases[u, 1]], axis=1)
        state = pl.pallas_call(
            post_kernel,
            out_shape=jax.ShapeDtypeStruct((ILO, IHI, TC, C), BF),
            scratch_shapes=[pltpu.VMEM((C * SP, C), F32)],
            name="post",
        )(products, state, gate, gb_out, w_out[u])
    return state.reshape(TR, TC, C)


def solution(mesh):
    placed = (P("row", "col", None), P(), P(), P(), P(), P())
    return jax.shard_map(
        body, mesh=mesh, in_specs=placed, out_specs=P("row", "col", None), check_vma=False
    )
```

time: 236 us -> 200 us (0.85)
  Pallas kernels: 0 us -> 50.1 us
  waiting for transfers between devices: 119 us -> 77.3 us
  matrix products: 35.8 us -> 5.92 us
  local copies, waits for them, and re-layouts: 33.1 us -> 21.8 us
  starting transfers between devices: 35.5 us -> 25.1 us
  other arithmetic: 11 us -> 18.1 us
    pallas_call x0 -> x6, Pallas kernels: none -> 50.1 us  [the longest x2 20.9 us: body(): pl.pallas_call(functools.partial(tri_kernel, incoming=u == 1), out_shape=...]
    all_to_all x6 -> x4, waiting for transfers between devices: 119 us -> 77.3 us  [the longest x2 44.1 us: body(): factors = lax.all_to_all(factors, axes, 0, 0, tiled=True)]
    dot_general x14 -> x2, matrix products: 35.8 us -> 5.92 us  [body(): jnp.dot(normed, w[:, 4 * C:], preferred_element_type=F32)]
    another operation x12 -> x3, local copies, waits for them, and re-layouts: 18.7 us -> 2.9 us  [body(): gb_out = jnp.stack([gains[u, 1], biases[u, 1]], axis=1)]
    all_to_all x6 -> x4, starting transfers between devices: 35.5 us -> 25.1 us  [the longest x2 16 us: body(): factors = lax.all_to_all(factors, axes, 0, 0, tiled=True)]
    transpose x6 -> x3, local copies, waits for them, and re-layouts: 9.49 us -> 2.39 us  [the longest x2 2.29 us: body(): w_t = w[:, :4 * C].T]
    unnamed x14 -> x28, local copies, waits for them, and re-layouts: 0.89 us -> 6.88 us
    convert_element_type x2 -> x3, other arithmetic: 0.03 us -> 5.17 us  [the longest x2 5.15 us: body(): norm_rows(state.reshape(-1, C), gains[u, 0], biases[u, 0]).astype(BF)]
  transfers between devices with their start and end apart: 6 -> 4, of which waited for: 6 -> 4; matrix products, arithmetic and copies ran while one was open for 13% -> 17% of each run, Pallas kernels for 0% -> 0%
where the time goes in v1:
time: 200 us; the launch traced here: 198 us
  waiting for transfers between devices  77.3 us (39%)
  Pallas kernels  50.1 us (25%)
  starting transfers between devices  25.1 us (13%)
  local copies, waits for them, and re-layouts  21.8 us (11%)
  other arithmetic  18.1 us (9%)
  matrix products  5.92 us (3%)
    all_to_all x2, waiting for transfers between devices, body(): factors = lax.all_to_all(factors, axes, 0, 0, tiled=True)  44.1 us
    all_to_all x2, waiting for transfers between devices, body(): products = lax.all_to_all(products, axes, 0, 0, tiled=True)  33.2 us
    pallas_call x2, Pallas kernels, body(): pl.pallas_call(functools.partial(tri_kernel, incoming=u == 1), out_shape=...  20.9 us
    all_to_all x2, starting transfers between devices, body(): factors = lax.all_to_all(factors, axes, 0, 0, tiled=True)  16 us
    pallas_call x2, Pallas kernels, body(): pl.pallas_call(pre_kernel, out_shape=jax.ShapeDtypeStruct((C, 2 * NQ, C),...  14.6 us
    pallas_call x2, Pallas kernels, body(): pl.pallas_call(post_kernel, out_shape=jax.ShapeDtypeStruct((ILO, IHI, TC,...  14.6 us
    all_to_all x2, starting transfers between devices, body(): products = lax.all_to_all(products, axes, 0, 0, tiled=True)  9.05 us
    unnamed x28, local copies, waits for them, and re-layouts  6.88 us
  transfers between devices with their start and end apart: 4, of which 4 were waited for; matrix products, arithmetic and copies ran while one was open for 17% of the time, Pallas kernels for 0%

profile of v1, /device:TPU:1, one launch (start us, length us, event | category | flops | bytes accessed | tf_op | source)
XLA Modules:
  0.0 198.4 jit_solution(5029303657877461637)
XLA Ops:
  0.0 1.7 fusion.25
  5.2 1.4 slice_bitcast_fusion.4
  7.2 7.3 %pre.2 = bf16[128,72,128]{2,1,0:T(8,128)(2,1)} custom-call(bf16[4,12,96,128]{3,2,1,0:T(8,128)(2,1)} %bitcast.62, bf16[512,128]{1,0:T(8,128)(2,1)} %slice_bitcast_fusion.1.w_ref, f32[2,128]{1,0:T(2,128)} %pad_maximum_fusion.gb_ref, f32[36,128]{1,0:T(8,128)} %mul.72.mask_ref), custom_call_target="tpu_custom_call" | custom-call | tf_op jit(solution)/shard_map/pre/pallas_call | solution.py:178
  14.5 11.5 %all-to-all-start = ((bf16[128,72,128]{2,1,0:T(8,128)(2,1)}), bf16[128,72,128]{2,1,0:T(8,128)(2,1)S(1)}, u32[]{:S(2)}, u32[]{:S(2)}) async-start(bf16[128,72,128]{2,1,0:T(8,128)(2,1)} %pre.2), calls=%async_computation | async-start | bytes 4718592 | tf_op jit(solution)/shard_map/all_to_all | solution.py:184
  27.1 1.4 div.45
  28.5 2.3 %multiply_reduce_fusion.1 = f32[48,96]{1,0:T(8,128)S(1)} fusion(bf16[48,96,128]{2,1,0:T(8,128)(2,1)S(1)} %copy-done.1, f32[48,96]{1,0:T(8,128)} %broadcast_multiply_fusion.2), kind=kLoop, calls=%fused_computation.19 | loop fusion | flops 2354688 | bytes 1216512 | tf_op jit(solution)/shard_map/reduce_sum | solution.py:38
  31.5 1.4 rsqrt.23
  34.3 1.7 copy.32
  36.0 1.3 pad_maximum_fusion.2.gb_ref
  37.3 1.4 slice_bitcast_fusion.2
  38.7 1.6 slice_bitcast_fusion.w_ref
  40.3 19.0 %all-to-all-done.in_ref = bf16[128,72,128]{2,1,0:T(8,128)(2,1)S(1)} async-done(((bf16[128,72,128]{2,1,0:T(8,128)(2,1)}), bf16[128,72,128]{2,1,0:T(8,128)(2,1)S(1)}, u32[]{:S(2)}, u32[]{:S(2)}) %all-to-all-start) | async-done | bytes 2359328 | tf_op jit(solution)/shard_map/all_to_all | solution.py:184
  59.3 1.4 copy-done.2
  60.7 10.4 %tri.2 = bf16[128,36,128]{2,1,0:T(8,128)(2,1)} custom-call(bf16[128,72,128]{2,1,0:T(8,128)(2,1)} %copy-done.2), custom_call_target="tpu_custom_call" | custom-call | tf_op jit(solution)/shard_map/tri/pallas_call | solution.py:188
  71.1 4.5 %all-to-all-start.1 = ((bf16[128,36,128]{2,1,0:T(8,128)(2,1)}), bf16[128,36,128]{2,1,0:T(8,128)(2,1)S(1)}, u32[]{:S(2)}, u32[]{:S(2)}) async-start(bf16[128,36,128]{2,1,0:T(8,128)(2,1)} %tri.2), calls=%async_computation.1 | async-start | bytes 2621440 | tf_op jit(solution)/shard_map/all_to_all | solution.py:198
  75.7 2.5 %fusion.13 = bf16[4608,128]{1,0:T(8,128)(2,1)S(1)} fusion(bf16[48,96,128]{2,1,0:T(8,128)(2,1)S(1)} %copy-done.1, f32[128]{0:T(128)S(1)} %get-tuple-element.16, f32[128]{0:T(128)S(1)} %copy-done.11, f32[4608]{0:T(1024)S(1)} %copy-done.8, f32[4608]{0:T(1024)S(1)} %copy-done.7), kind=kLoop, calls=%fused_computation.17 | loop fusion | flops 3538944 | bytes 2397184 | tf_op jit(solution)/shard_map/convert_element_type | solution.py:185
  78.2 3.0 %fusion.4 = f32[4608,128]{1,0:T(8,128)} fusion(bf16[4608,128]{1,0:T(8,128)(2,1)S(1)} %fusion.13, bf16[128,640]{0,1:T(8,128)(2,1)} %bitcast.67), kind=kOutput, calls=%fused_computation.6 | convolution fusion | flops 152764416 | bytes 3571712 | tf_op jit(solution)/shard_map/dot_general | solution.py:186
  81.2 16.7 %all-to-all-done.1.in_ref = bf16[128,36,128]{2,1,0:T(8,128)(2,1)S(1)} async-done(((bf16[128,36,128]{2,1,0:T(8,128)(2,1)}), bf16[128,36,128]{2,1,0:T(8,128)(2,1)S(1)}, u32[]{:S(2)}, u32[]{:S(2)}) %all-to-all-start.1) | async-done | bytes 1179680 | tf_op jit(solution)/shard_map/all_to_all | solution.py:198
  98.9 7.3 %post.2.z_ref = bf16[4,12,96,128]{3,2,1,0:T(8,128)(2,1)} custom-call(bf16[128,36,128]{2,1,0:T(8,128)(2,1)} %copy-done.5, bf16[4,12,96,128]{3,2,1,0:T(8,128)(2,1)} %bitcast.63, f32[4,12,96,128]{3,2,1,0:T(8,128)} %bitcast.65, f32[128,2]{1,0:T(8,128)} %copy.28.gb_ref, bf16[128,128]{1,0:T(8,128)(2,1)} %get-tuple-element.8.w_ref), custom_call_target="tpu_custom_call" | custom-call | tf_op jit(solution)/shard_map/post/pallas_call | solution.py:200
  106.2 7.3 %pre.3 = bf16[128,72,128]{2,1,0:T(8,128)(2,1)} custom-call(bf16[4,12,96,128]{3,2,1,0:T(8,128)(2,1)} %post.2.z_ref, bf16[512,128]{1,0:T(8,128)(2,1)} %slice_bitcast_fusion.w_ref, f32[2,128]{1,0:T(2,128)} %pad_maximum_fusion.2.gb_ref, f32[36,128]{1,0:T(8,128)} %mul.72.mask_ref), custom_call_target="tpu_custom_call" | custom-call | tf_op jit(solution)/shard_map/pre/pallas_call | solution.py:178
  113.5 4.5 %all-to-all-start.2 = ((bf16[128,72,128]{2,1,0:T(8,128)(2,1)}), bf16[128,72,128]{2,1,0:T(8,128)(2,1)S(1)}, u32[]{:S(2)}, u32[]{:S(2)}) async-start(bf16[128,72,128]{2,1,0:T(8,128)(2,1)} %pre.3), calls=%async_computation.2 | async-start | bytes 4718592 | tf_op jit(solution)/shard_map/all_to_all | solution.py:184
  120.6 1.4 div.49
  122.0 2.3 %multiply_reduce_fusion = f32[4,12,96]{2,1,0:T(8,128)S(1)} fusion(bf16[4,12,96,128]{3,2,1,0:T(8,128)(2,1)S(1)} %copy-done, f32[4,12,96]{2,1,0:T(8,128)} %broadcast_multiply_fusion.1), kind=kLoop, calls=%fused_computation.18 | loop fusion | flops 2354688 | bytes 1216512 | tf_op jit(solution)/shard_map/reduce_sum | solution.py:38
  125.0 1.4 rsqrt.25
  126.4 25.0 %all-to-all-done.2.in_ref = bf16[128,72,128]{2,1,0:T(8,128)(2,1)S(1)} async-done(((bf16[128,72,128]{2,1,0:T(8,128)(2,1)}), bf16[128,72,128]{2,1,0:T(8,128)(2,1)S(1)}, u32[]{:S(2)}, u32[]{:S(2)}) %all-to-all-start.2) | async-done | bytes 2359328 | tf_op jit(solution)/shard_map/all_to_all | solution.py:184
  151.5 1.4 copy-done.3
  152.9 10.4 %tri.3 = bf16[128,36,128]{2,1,0:T(8,128)(2,1)} custom-call(bf16[128,72,128]{2,1,0:T(8,128)(2,1)} %copy-done.3), custom_call_target="tpu_custom_call" | custom-call | tf_op jit(solution)/shard_map/tri/pallas_call | solution.py:188
  163.3 4.5 %all-to-all-start.3 = ((bf16[128,36,128]{2,1,0:T(8,128)(2,1)}), bf16[128,36,128]{2,1,0:T(8,128)(2,1)S(1)}, u32[]{:S(2)}, u32[]{:S(2)}) async-start(bf16[128,36,128]{2,1,0:T(8,128)(2,1)} %tri.3), calls=%async_computation.3 | async-start | bytes 2621440 | tf_op jit(solution)/shard_map/all_to_all | solution.py:198
  167.9 2.6 %fusion.9 = bf16[4608,128]{1,0:T(8,128)(2,1)S(1)} fusion(bf16[4,12,96,128]{3,2,1,0:T(8,128)(2,1)S(1)} %copy-done, f32[128]{0:T(128)S(1)} %get-tuple-element.17, f32[128]{0:T(128)S(1)} %get-tuple-element.24, f32[4608]{0:T(1024)S(1)} %copy-done.10, f32[4608]{0:T(1024)S(1)} %copy-done.9), kind=kLoop, calls=%fused_computation.12 | loop fusion | flops 3538944 | bytes 2397184 | tf_op jit(solution)/shard_map/convert_element_type | solution.py:185
  170.5 3.0 %fusion.5 = f32[4608,128]{1,0:T(8,128)} fusion(bf16[4608,128]{1,0:T(8,128)(2,1)S(1)} %fusion.9, bf16[128,640]{0,1:T(8,128)(2,1)} %bitcast.69), kind=kOutput, calls=%fused_computation.7 | convolution fusion | flops 152764416 | bytes 3571712 | tf_op jit(solution)/shard_map/dot_general | solution.py:186
  173.5 16.6 %all-to-all-done.3.in_ref = bf16[128,36,128]{2,1,0:T(8,128)(2,1)S(1)} async-done(((bf16[128,36,128]{2,1,0:T(8,128)(2,1)}), bf16[128,36,128]{2,1,0:T(8,128)(2,1)S(1)}, u32[]{:S(2)}, u32[]{:S(2)}) %all-to-all-start.3) | async-done | bytes 1179680 | tf_op jit(solution)/shard_map/all_to_all | solution.py:198
  191.1 7.3 %post.3 = bf16[4,12,96,128]{3,2,1,0:T(8,128)(2,1)} custom-call(bf16[128,36,128]{2,1,0:T(8,128)(2,1)} %copy-done.4, bf16[4,12,96,128]{3,2,1,0:T(8,128)(2,1)} %post.2.z_ref, f32[4,12,96,128]{3,2,1,0:T(8,128)} %bitcast.64, f32[128,2]{1,0:T(8,128)} %copy.30.gb_ref, bf16[128,128]{1,0:T(8,128)(2,1)} %get-tuple-element.7.w_ref), custom_call_target="tpu_custom_call" | custom-call | tf_op jit(solution)/shard_map/post/pallas_call | solution.py:200
  (48 shorter events, 12.5 us)
Async XLA Ops:
  1.9 5.3 %copy-start.6 = (bf16[1,128,640]{1,2,0:T(8,128)(2,1)}, bf16[1,128,640]{1,2,0:T(8,128)(2,1)S(1)}, u32[]{:S(2)}) copy-start(bf16[1,128,640]{1,2,0:T(8,128)(2,1)S(1)} %copy.31) | copy-start | bytes 491524
  14.5 11.5 %copy-start.1 = (bf16[48,96,128]{2,1,0:T(8,128)(2,1)S(1)}, bf16[48,96,128]{2,1,0:T(8,128)(2,1)}, u32[]{:S(2)}) copy-start(bf16[48,96,128]{2,1,0:T(8,128)(2,1)} %param.6) | copy-start | bytes 3538948
  14.5 44.8 %all-to-all-start = ((bf16[128,72,128]{2,1,0:T(8,128)(2,1)}), bf16[128,72,128]{2,1,0:T(8,128)(2,1)S(1)}, u32[]{:S(2)}, u32[]{:S(2)}) async-start(bf16[128,72,128]{2,1,0:T(8,128)(2,1)} %pre.2), calls=%async_computation | async-start | bytes 4718592 | tf_op jit(solution)/shard_map/all_to_all | solution.py:184
  40.3 35.4 %copy-start.11 = (f32[128]{0:T(128)S(1)}, f32[128]{0:T(128)}, u32[]{:S(2)}) copy-start(f32[128]{0:T(128)} %get-tuple-element.25) | copy-start | bytes 1540
  59.3 1.4 copy-start.2
  71.1 4.5 %copy-start.7 = (f32[4608]{0:T(1024)S(1)}, f32[4608]{0:T(1024)}, u32[]{:S(2)}) copy-start(f32[4608]{0:T(1024)} %div.45) | copy-start | bytes 55300
  71.1 4.6 %copy-start.8 = (f32[4608]{0:T(1024)S(1)}, f32[4608]{0:T(1024)}, u32[]{:S(2)}) copy-start(f32[4608]{0:T(1024)} %rsqrt.23) | copy-start | bytes 55300
  71.1 26.7 %all-to-all-start.1 = ((bf16[128,36,128]{2,1,0:T(8,128)(2,1)}), bf16[128,36,128]{2,1,0:T(8,128)(2,1)S(1)}, u32[]{:S(2)}, u32[]{:S(2)}) async-start(bf16[128,36,128]{2,1,0:T(8,128)(2,1)} %tri.2), calls=%async_computation.1 | async-start | bytes 2621440 | tf_op jit(solution)/shard_map/all_to_all | solution.py:198
  97.8 1.1 copy-start.5
  113.5 4.6 %copy-start.12 = (f32[128,1]{0,1:T(1,128)S(1)}, f32[128,1]{0,1:T(1,128)}, u32[]{:S(2)}) copy-start(f32[128,1]{0,1:T(1,128)} %get-tuple-element.15) | copy-start | bytes 1540
  113.5 5.9 %copy-start = (bf16[4,12,96,128]{3,2,1,0:T(8,128)(2,1)S(1)}, bf16[4,12,96,128]{3,2,1,0:T(8,128)(2,1)}, u32[]{:S(2)}) copy-start(bf16[4,12,96,128]{3,2,1,0:T(8,128)(2,1)} %post.2.z_ref) | copy-start | bytes 3538948
  113.5 38.0 %all-to-all-start.2 = ((bf16[128,72,128]{2,1,0:T(8,128)(2,1)}), bf16[128,72,128]{2,1,0:T(8,128)(2,1)S(1)}, u32[]{:S(2)}, u32[]{:S(2)}) async-start(bf16[128,72,128]{2,1,0:T(8,128)(2,1)} %pre.3), calls=%async_computation.2 | async-start | bytes 4718592 | tf_op jit(solution)/shard_map/all_to_all | solution.py:184
  151.5 1.4 copy-start.3
  163.3 4.5 %copy-start.9 = (f32[4608]{0:T(1024)S(1)}, f32[4608]{0:T(1024)}, u32[]{:S(2)}) copy-start(f32[4608]{0:T(1024)} %div.49) | copy-start | bytes 55300
  163.3 4.5 %copy-start.10 = (f32[4608]{0:T(1024)S(1)}, f32[4608]{0:T(1024)}, u32[]{:S(2)}) copy-start(f32[4608]{0:T(1024)} %rsqrt.25) | copy-start | bytes 55300
  163.3 26.7 %all-to-all-start.3 = ((bf16[128,36,128]{2,1,0:T(8,128)(2,1)}), bf16[128,36,128]{2,1,0:T(8,128)(2,1)S(1)}, u32[]{:S(2)}, u32[]{:S(2)}) async-start(bf16[128,36,128]{2,1,0:T(8,128)(2,1)} %tri.3), calls=%async_computation.3 | async-start | bytes 2621440 | tf_op jit(solution)/shard_map/all_to_all | solution.py:198
  190.0 1.1 copy-start.4

commit v2 on v0

v2 whole, which is shorter than its diff:
```python
import functools
import jax
import jax.numpy as jnp
from jax import lax
from jax.experimental import pallas as pl
from jax.experimental.pallas import tpu as pltpu
from jax.sharding import PartitionSpec as P

N = 768
C = 128
ROWS, COLS = 16, 8
TR, TC = N // ROWS, N // COLS
KHI, KLO = 3, 32
NQ = 36
SA, SP = 72, 40
STORES = 8
BF, F32 = jnp.bfloat16, jnp.float32


def norm_rows(z, gain, bias):
    wide = z.astype(F32)
    mean = jnp.mean(wide, axis=1, keepdims=True)
    centred = wide - mean
    var = jnp.mean(centred * centred, axis=1, keepdims=True)
    return centred * lax.rsqrt(var + 1e-05) * gain + bias


def sigmoid(x):
    return 0.5 * jnp.tanh(0.5 * x) + 0.5


def pick(parts, odd, high):
    return jnp.where(high, jnp.where(odd, parts[3], parts[2]), jnp.where(odd, parts[1], parts[0]))


def swap_blocks(x):
    lane = lax.broadcasted_iota(jnp.int32, x[0].shape, 1)
    odd, high = (lane // 32) % 2 == 1, lane >= 64
    skew = [pick([x[(b + d) % 4] for b in range(4)], odd, high) for d in range(4)]
    turned = [skew[0]] + [pltpu.roll(skew[d], 32 * d, 1) for d in range(1, 4)]
    return [pick([turned[(b - a) % 4] for b in range(4)], odd, high) for a in range(4)]


def tri_kernel(in_ref, out_hbm, mlb, mrb, tri, stage, sems, *, incoming):
    top = lax.broadcasted_iota(jnp.int32, (8, C), 0) < 4

    def gather(r, carry):
        whole = [in_ref[r * COLS + c].astype(F32) for c in range(COLS)]
        for v in range(6):
            x = []
            for b in range(4):
                c, h = divmod(4 * v + b, KHI)
                x.append(whole[c][h * 24:(h + 1) * 24, :])
            y = swap_blocks(x)
            tail = [z[16:24] for z in y]
            left, right = [z[0:8] for z in y], [z[8:16] for z in y]
            for a in (0, 2):
                left.append(jnp.where(top, tail[a], pltpu.roll(tail[a + 1], 4, 0)))
                right.append(jnp.where(top, pltpu.roll(tail[a], 4, 0), tail[a + 1]))
            rows, lanes = pl.ds(pl.multiple_of(r * TR, TR), TR), slice(v * C, (v + 1) * C)
            mlb[rows, lanes] = jnp.concatenate(left, axis=0).astype(BF)
            mrb[rows, lanes] = jnp.concatenate(right, axis=0).astype(BF)
        return carry

    lax.fori_loop(0, ROWS, gather, 0, unroll=2)
    for m in range(2):
        cut = slice(m * 384, (m + 1) * 384)
        if incoming:
            tri[cut, :] = lax.dot_general(
                mlb[:, cut], mrb[...], (((0,), (0,)), ((), ())), preferred_element_type=F32)
        else:
            tri[cut, :] = lax.dot_general(
                mlb[cut, :], mrb[...], (((1,), (1,)), ((), ())), preferred_element_type=F32)

    def copy_out(r):
        dests = pl.ds(r * 2 * COLS, 2 * COLS)
        return pltpu.make_async_copy(stage.at[dests], out_hbm.at[dests], sems.at[r])

    def scatter(t, carry):
        rs = (2 * t, 2 * t + 1)
        base = [pl.multiple_of(r * TR, TR) for r in rs]
        main, tail = ([], []), []
        for v in range(6):
            lanes = slice(v * C, (v + 1) * C)
            for e in range(2):
                main[e].extend(swap_blocks([tri[pl.ds(base[e] + 8 * a, 8), lanes] for a in range(4)]))
            ends = []
            for a in (32, 40):
                p, q = (tri[pl.ds(base[e] + a, 8), lanes] for e in range(2))
                ends.append(jnp.where(top, p, pltpu.roll(q, 4, 0)))
                ends.append(jnp.where(top, pltpu.roll(p, 4, 0), q))
            tail += swap_blocks(ends)
        for c in range(COLS):
            j = tail[KHI * c:KHI * c + KHI]
            last = (
                [jnp.where(top, j[0], pltpu.roll(j[1], 4, 0)), j[2]],
                [jnp.where(top, pltpu.roll(j[0], 4, 0), j[1]), pltpu.roll(j[2], 4, 0)],
            )
            for e in range(2):
                block = jnp.concatenate(main[e][KHI * c:KHI * c + KHI] + last[e], axis=0)
                stage[rs[e] * COLS + c] = block.astype(BF)
        copy_out(t).start()
        return carry

    lax.fori_loop(0, ROWS // 2, scatter, 0)

    def finish(r, carry):
        copy_out(r).wait()
        return carry

    lax.fori_loop(0, ROWS // 2, finish, 0)


def place(g):
    h, part = g // 3, g % 3
    tail = part == 2
    row = jnp.where(tail, TR - 16, 4 * part)
    step = jnp.where(tail, 4, 8)
    factor_rows = [h * 24 + jnp.where(tail, 16 + 4 * side, 8 * side + 4 * part) for side in range(2)]
    product_row = jnp.where(tail, 24 + 4 * h, 8 * h + 4 * part)
    return h, row, step, factor_rows, product_row


def copies(src, dst, sems, cuts):
    return [pltpu.make_async_copy(src.at[k], dst.at[k], sems.at[n]) for n, k in enumerate(cuts)]


def column_cuts():
    return [(slice(None), pl.ds(h * KLO, KLO)) for h in range(KHI)]


def wait_column(g, *lists):
    for h in range(KHI):
        @pl.when(g == 3 * h)
        def _():
            for some in lists:
                some[h].wait()


def load_chunk(z, row, step, h):
    cut = pl.ds(pl.multiple_of(h * KLO, KLO), KLO)
    return jnp.concatenate([z[row + a * step, cut, :] for a in range(4)], axis=0)


def store_chunk(z, row, step, h, value):
    cut = pl.ds(pl.multiple_of(h * KLO, KLO), KLO)
    for a in range(4):
        z[row + a * step, cut, :] = value[a * KLO:(a + 1) * KLO]


def projector(chain, w, gains, biases, scr, u):
    row, col = lax.axis_index("row"), lax.axis_index("col")
    live_rows = chain[row // 2] - TR * (row % 2)
    live_cols = chain[col]
    gain, bias = gains[u, 0:1, :], biases[u, 0:1, :]
    w_t = [w[u, :, k * C:(k + 1) * C].T for k in range(4)]
    lane = lax.broadcasted_iota(jnp.int32, (1, C), 1)

    def project(chunks, h, first, step, factor_rows):
        lane_row, lane_col = lane // KLO * step + first, lane % KLO + h * KLO
        for half in range(2):
            es = (2 * half, 2 * half + 1)
            normed = jnp.concatenate([norm_rows(chunks[e], gain, bias).astype(BF) for e in es], axis=0)
            mask = jnp.concatenate(
                [((lane_row + e < live_rows) & (lane_col < live_cols)).astype(F32) for e in es], axis=1)
            for side in range(2):
                value, gate = (
                    lax.dot_general(
                        w_t[2 * side + k], normed, (((1,), (1,)), ((), ())), preferred_element_type=F32)
                    for k in range(2)
                )
                edges = mask * sigmoid(gate) * value
                for n, e in enumerate(es):
                    scr[pl.ds(factor_rows[side] + e, C, stride=SA), :] = edges[:, n * C:(n + 1) * C]

    return project


def send_factors(scr, stage, out, sems):
    per = C // STORES
    outs = copies(stage, out, sems, [pl.ds(n * per, per) for n in range(STORES)])

    def cast(s, carry):
        stage[s] = scr[pl.ds(pl.multiple_of(s * SA, 8), SA), :].astype(BF)
        return carry

    for n in range(STORES):
        lax.fori_loop(n * per, (n + 1) * per, cast, 0, unroll=4)
        outs[n].start()
    return outs


def pre_kernel(chain_hbm, z_hbm, w_hbm, gain_hbm, bias_hbm, out_hbm,
               chain, z, w, gains, biases, scr, stage, in_sems, z_sems, out_sems):
    small = [pltpu.make_async_copy(a, b, in_sems.at[n]) for n, (a, b) in enumerate(
        ((chain_hbm, chain), (w_hbm, w), (gain_hbm, gains), (bias_hbm, biases)))]
    z_in = copies(z_hbm, z, z_sems, column_cuts())
    for one in small + z_in:
        one.start()
    for one in small:
        one.wait()
    project = projector(chain, w, gains, biases, scr, 0)

    def step(g, carry):
        wait_column(g, z_in)
        h, row, gap, factor_rows, _ = place(g)
        project([load_chunk(z, row + e, gap, h) for e in range(4)], h, row, gap, factor_rows)
        return carry

    lax.fori_loop(0, 9, step, 0)
    for one in send_factors(scr, stage, out_hbm, out_sems):
        one.wait()


def post_parts(prod, z_hbm, gate_hbm, gains, biases, w_out, z, gate, wide, z_sems, gate_sems, u):
    z_in = copies(z_hbm, z, z_sems, column_cuts())
    gate_in = copies(gate_hbm, gate, gate_sems, column_cuts())
    for one in z_in + gate_in:
        one.start()
    gain = jnp.broadcast_to(gains[u, 1:2, :], (C, C)).T
    bias = jnp.broadcast_to(biases[u, 1:2, :], (C, C)).T

    def widen(s, carry):
        wide[pl.ds(pl.multiple_of(s * SP, 8), SP), :] = prod[s].astype(F32)
        return carry

    lax.fori_loop(0, C, widen, 0, unroll=4)

    def chunk(g, e):
        h, row, gap, _, product_row = place(g)
        x = wide[pl.ds(product_row + e, C, stride=SP), :]
        mean = jnp.mean(x, axis=0, keepdims=True)
        centred = x - mean
        var = jnp.mean(centred * centred, axis=0, keepdims=True)
        normed = (centred * lax.rsqrt(var + 1e-05) * gain + bias).astype(BF)
        mixed = lax.dot_general(
            normed, w_out[u], (((0,), (0,)), ((), ())), preferred_element_type=F32)
        old = load_chunk(z, row + e, gap, h).astype(F32)
        return (old + load_chunk(gate, row + e, gap, h) * mixed).astype(BF)

    return z_in, gate_in, chunk


def mid_kernel(chain, prod, z_hbm, gate_hbm, w, gains, biases, w_out, z_out_hbm, out_hbm,
               z, gate, wide, z_out, scr, stage, z_sems, gate_sems, zo_sems, out_sems):
    z_in, gate_in, chunk = post_parts(
        prod, z_hbm, gate_hbm, gains, biases, w_out, z, gate, wide, z_sems, gate_sems, 0)
    project = projector(chain, w, gains, biases, scr, 1)
    z_done = copies(z_out, z_out_hbm, zo_sems, column_cuts())

    def step(g, carry):
        wait_column(g, z_in, gate_in)
        h, row, gap, factor_rows, _ = place(g)
        new = [chunk(g, e) for e in range(4)]
        for e in range(4):
            store_chunk(z_out, row + e, gap, h, new[e])
        project(new, h, row, gap, factor_rows)
        for k in range(KHI):
            @pl.when(g == 3 * k + 2)
            def _():
                z_done[k].start()
        return carry

    lax.fori_loop(0, 9, step, 0)
    for one in send_factors(scr, stage, out_hbm, out_sems) + z_done:
        one.wait()


def post_kernel(prod, z_hbm, gate_hbm, gains, biases, w_out, z_out_hbm,
                z, gate, wide, z_out, z_sems, gate_sems, zo_sems):
    z_in, gate_in, chunk = post_parts(
        prod, z_hbm, gate_hbm, gains, biases, w_out, z, gate, wide, z_sems, gate_sems, 1)
    z_done = copies(z_out, z_out_hbm, zo_sems, column_cuts())

    def step(g, carry):
        wait_column(g, z_in, gate_in)
        h, row, gap, _, _ = place(g)
        for e in range(4):
            store_chunk(z_out, row + e, gap, h, chunk(g, e))
        for k in range(KHI):
            @pl.when(g == 3 * k + 2)
            def _():
                z_done[k].start()
        return carry

    lax.fori_loop(0, 9, step, 0)
    for one in z_done:
        one.wait()


HBM = pl.BlockSpec(memory_space=pltpu.HBM)
VMEM = pl.BlockSpec(memory_space=pltpu.VMEM)
SMEM = pl.BlockSpec(memory_space=pltpu.SMEM)
FACTORS, PRODUCTS, STATE = ((C, 2 * NQ, C), BF), ((C, SP, C), BF), ((TR, TC, C), BF)


def call(kernel, name, outs, scratch, sems, limit, in_specs):
    shapes = [pltpu.HBM(*o) for o in outs]
    run = pl.pallas_call(
        kernel,
        out_shape=shapes if len(shapes) > 1 else shapes[0],
        in_specs=in_specs,
        out_specs=[HBM] * len(shapes) if len(shapes) > 1 else HBM,
        scratch_shapes=list(scratch) + [pltpu.SemaphoreType.DMA((n,)) for n in sems],
        compiler_params=pltpu.CompilerParams(vmem_limit_bytes=limit << 20),
        name=name,
    )

    def placed(*args):
        return run(*(
            pltpu.with_memory_space_constraint(a, s.memory_space)
            if s is HBM or (s is VMEM and a.size > N * N) else a
            for a, s in zip(args, in_specs)
        ))

    return placed


def kernels():
    V = pltpu.VMEM
    send = [V((C * SA, C), F32), V(*FACTORS)]
    pre = call(
        pre_kernel, "pre", [FACTORS],
        [pltpu.SMEM((8,), jnp.int32), V(*STATE), V((2, C, 5 * C), BF), V((2, 2, C), F32), V((2, 2, C), F32)] + send,
        [4, KHI, STORES], 20, [HBM] * 5)
    tri = [
        call(
            functools.partial(tri_kernel, incoming=u == 1), "tri", [PRODUCTS],
            [V((N, N), BF), V((N, N), BF), V((N, N), F32), V(*PRODUCTS)], [ROWS // 2], 20, [VMEM])
        for u in range(2)
    ]
    take = [V(*STATE), V(STATE[0], F32), V((C * SP, C), F32), V(*STATE)]
    mid = call(
        mid_kernel, "mid", [STATE, FACTORS], take + send, [KHI, KHI, KHI, STORES], 26,
        [SMEM, VMEM] + [HBM] * 2 + [VMEM] * 4)
    post = call(
        post_kernel, "post", [STATE], take, [KHI, KHI, KHI], 16, [VMEM] + [HBM] * 2 + [VMEM] * 3)
    return pre, tri, mid, post


def output_gate(state, w_in, gains, biases, u):
    normed = norm_rows(state.reshape(-1, C), gains[u, 0], biases[u, 0]).astype(BF)
    gate = jax.nn.sigmoid(jnp.dot(normed, w_in[u, :, 4 * C:], preferred_element_type=F32))
    return gate.reshape(state.shape)


def body(pair, chain_lengths, gains, biases, w_in, w_out):
    def exchange(blocks):
        return lax.all_to_all(blocks, ("row", "col"), 0, 0, tiled=True)

    pre, tri, mid, post = kernels()
    factors = exchange(pre(chain_lengths, pair, w_in, gains, biases))
    gate = output_gate(pair, w_in, gains, biases, 0)
    products = exchange(tri[0](factors))
    state, factors = mid(chain_lengths, products, pair, gate, w_in, gains, biases, w_out)
    factors = exchange(factors)
    gate = output_gate(state, w_in, gains, biases, 1)
    products = exchange(tri[1](factors))
    return post(products, state, gate, gains, biases, w_out)


def solution(mesh):
    placed = (P("row", "col", None), P(), P(), P(), P(), P())
    return jax.shard_map(
        body, mesh=mesh, in_specs=placed, out_specs=P("row", "col", None), check_vma=False
    )
```

time: 236 us -> 169 us (0.72)
  local copies, waits for them, and re-layouts: 33.1 us -> 0.05 us
  Pallas kernels: 0 us -> 32 us
  matrix products: 35.8 us -> 4.39 us
  waiting for transfers between devices: 119 us -> 95.6 us
  starting transfers between devices: 35.5 us -> 25 us
    pallas_call x0 -> x5, Pallas kernels: none -> 32 us  [placed(): run(*(pltpu.with_memory_space_constraint(a, s.memory_space) if s is HBM o...]
    dot_general x14 -> x2, matrix products: 35.8 us -> 4.39 us  [output_gate(): jnp.dot(normed, w_in[u, :, 4 * C:], preferred_element_type=F32)]
    all_to_all x6 -> x4, waiting for transfers between devices: 119 us -> 95.6 us  [exchange(): return lax.all_to_all(blocks, ('row', 'col'), 0, 0, tiled=True)]
    another operation x12 -> x0, local copies, waits for them, and re-layouts: 18.7 us -> none  [the longest x4 9.18 us: exchange_both(): blocks = blocks.reshape(-1, *inside)]
    all_to_all x6 -> x4, starting transfers between devices: 35.5 us -> 25 us  [exchange(): return lax.all_to_all(blocks, ('row', 'col'), 0, 0, tiled=True)]
    transpose x6 -> x0, local copies, waits for them, and re-layouts: 9.49 us -> none  [joined_along(): blocks = jnp.moveaxis(blocks, 0, dim)]
    reshape x2 -> x0, local copies, waits for them, and re-layouts: 3.98 us -> none  [joined_along(): blocks.reshape(*lengths[:dim], lengths[dim] * lengths[dim + 1], *lengths[...]
    convert_element_type x2, other arithmetic: 0.03 us -> 2.94 us  [output_gate(): norm_rows(state.reshape(-1, C), gains[u, 0], biases[u, 0]).astype(BF)]
  transfers between devices with their start and end apart: 6 -> 4, of which waited for: 6 -> 4; matrix products, arithmetic and copies ran while one was open for 13% -> 9% of each run, Pallas kernels for 0% -> 0%
where the time goes in v2:
time: 169 us; the launch traced here: 168 us
  waiting for transfers between devices  95.6 us (57%)
  Pallas kernels  32 us (19%)
  starting transfers between devices  25 us (15%)
  other arithmetic  10.9 us (6%)
  matrix products  4.39 us (3%)
    all_to_all x4, waiting for transfers between devices, exchange(): return lax.all_to_all(blocks, ('row', 'col'), 0, 0, tiled=True)  95.6 us
    pallas_call x5, Pallas kernels, placed(): run(*(pltpu.with_memory_space_constraint(a, s.memory_space) if s is HBM o...  32 us
    all_to_all x4, starting transfers between devices, exchange(): return lax.all_to_all(blocks, ('row', 'col'), 0, 0, tiled=True)  25 us
    reduce_sum x2, other arithmetic, norm_rows(): var = jnp.mean(centred * centred, axis=1, keepdims=True)  4.39 us
    dot_general x2, matrix products, output_gate(): jnp.dot(normed, w_in[u, :, 4 * C:], preferred_element_type=F32)  4.39 us
    reduce_sum x2, other arithmetic, norm_rows(): mean = jnp.mean(wide, axis=1, keepdims=True)  3.52 us
  transfers between devices with their start and end apart: 4, of which 4 were waited for; matrix products, arithmetic and copies ran while one was open for 9% of the time, Pallas kernels for 0%

profile of v2, /device:TPU:1, one launch (start us, length us, event | category | flops | bytes accessed | tf_op | source)
XLA Modules:
  0.0 168.1 jit_solution(2008264804960851526)
XLA Ops:
  0.0 7.8 %pre.1 = bf16[128,72,128]{2,1,0:T(8,128)(2,1)} custom-call(s32[8]{0:T(128)} %chain.1, bf16[48,96,128]{2,1,0:T(8,128)(2,1)} %z_hbm.3, bf16[2,128,640]{2,1,0:T(8,128)(2,1)} %w.1, f32[2,2,128]{2,1,0:T(2,128)} %gains.3, f32[2,2,128]{2,1,0:T(2,128)} %biases.3), custom_call_target="tpu_custom_call" | custom-call | tf_op jit(solution)/shard_map/pre/pallas_call | solution.py:310
  7.8 11.5 %all-to-all-start = ((bf16[128,72,128]{2,1,0:T(8,128)(2,1)}), bf16[128,72,128]{2,1,0:T(8,128)(2,1)S(1)}, u32[]{:S(2)}, u32[]{:S(2)}) async-start(bf16[128,72,128]{2,1,0:T(8,128)(2,1)} %pre.1), calls=%async_computation | async-start | bytes 4718592 | tf_op jit(solution)/shard_map/all_to_all | solution.py:349
  19.3 1.8 %convert_reduce_fusion.1 = f32[48,96]{1,0:T(8,128)S(1)} fusion(bf16[48,96,128]{2,1,0:T(8,128)(2,1)} %z_hbm.3), kind=kLoop, calls=%fused_computation.11 | loop fusion | flops 1175040 | bytes 1198080 | tf_op jit(solution)/shard_map/reduce_sum | solution.py:22
  21.1 31.5 %all-to-all-done.in_ref = bf16[128,72,128]{2,1,0:T(8,128)(2,1)S(1)} async-done(((bf16[128,72,128]{2,1,0:T(8,128)(2,1)}), bf16[128,72,128]{2,1,0:T(8,128)(2,1)S(1)}, u32[]{:S(2)}, u32[]{:S(2)}) %all-to-all-start) | async-done | bytes 2359328 | tf_op jit(solution)/shard_map/all_to_all | solution.py:349
  52.6 4.2 %tri.2 = bf16[128,40,128]{2,1,0:T(8,128)(2,1)} custom-call(bf16[128,72,128]{2,1,0:T(8,128)(2,1)S(1)} %all-to-all-done.in_ref), custom_call_target="tpu_custom_call" | custom-call | tf_op jit(solution)/shard_map/tri/pallas_call | solution.py:310
  56.8 0.0 copy-start.2
  56.8 0.0 copy-start.3
  56.8 0.0 copy-start.5
  56.8 4.5 %all-to-all-start.1 = ((bf16[128,40,128]{2,1,0:T(8,128)(2,1)}), bf16[128,40,128]{2,1,0:T(8,128)(2,1)S(1)}, u32[]{:S(2)}, u32[]{:S(2)}) async-start(bf16[128,40,128]{2,1,0:T(8,128)(2,1)} %tri.2), calls=%async_computation.1 | async-start | bytes 2621440 | tf_op jit(solution)/shard_map/all_to_all | solution.py:349
  61.4 0.0 copy-start
  61.4 2.7 %fusion.14 = f32[48,96]{1,0:T(8,128)S(1)} fusion(bf16[48,96,128]{2,1,0:T(8,128)(2,1)} %z_hbm.3, f32[48,96]{1,0:T(8,128)S(1)} %broadcast_multiply_fusion.1), kind=kLoop, calls=%fused_computation.20 | loop fusion | flops 2354688 | bytes 1216512 | tf_op jit(solution)/shard_map/reduce_sum | solution.py:24
  64.1 0.0 copy-done.2
  64.1 0.0 copy-done.3
  64.2 0.0 copy-done.5
  64.2 1.5 fusion.17
  65.7 0.0 copy-start.1
  65.7 0.0 copy-start.4
  65.7 2.2 %fusion.4 = f32[4608,128]{1,0:T(8,128)} fusion(bf16[4608,128]{1,0:T(8,128)(2,1)S(1)} %bitcast.22, bf16[2,128,640]{2,1,0:T(8,128)(2,1)S(1)} %copy-done), kind=kOutput, calls=%fused_computation.6 | convolution fusion | flops 152764416 | bytes 3571712 | tf_op jit(solution)/shard_map/dot_general | solution.py:343
  67.9 15.6 %all-to-all-done.1.prod = bf16[128,40,128]{2,1,0:T(8,128)(2,1)S(1)} async-done(((bf16[128,40,128]{2,1,0:T(8,128)(2,1)}), bf16[128,40,128]{2,1,0:T(8,128)(2,1)S(1)}, u32[]{:S(2)}, u32[]{:S(2)}) %all-to-all-start.1) | async-done | bytes 1310752 | tf_op jit(solution)/shard_map/all_to_all | solution.py:349
  83.5 0.0 copy-done.4
  83.5 10.8 %mid.1 = (bf16[48,96,128]{2,1,0:T(8,128)(2,1)}, bf16[128,72,128]{2,1,0:T(8,128)(2,1)}) custom-call(s32[8]{0:T(128)S(1)} %copy-done.4, bf16[128,40,128]{2,1,0:T(8,128)(2,1)S(1)} %all-to-all-done.1.prod, bf16[48,96,128]{2,1,0:T(8,128)(2,1)} %z_hbm.3, f32[48,96,128]{2,1,0:T(8,128)} %bitcast.20, bf16[2,128,640]{2,1,0:T(8,128)(2,1)S(1)} %copy-done, ...), custom_call_target="tpu_custom_call" | custom-call | tf_op jit(solution)/shard_map/mid/pallas_call | solution.py:310
  94.4 4.4 %all-to-all-start.2 = ((bf16[128,72,128]{2,1,0:T(8,128)(2,1)}), bf16[128,72,128]{2,1,0:T(8,128)(2,1)S(1)}, u32[]{:S(2)}, u32[]{:S(2)}) async-start(bf16[128,72,128]{2,1,0:T(8,128)(2,1)} %get-tuple-element.7), calls=%async_computation.2 | async-start | bytes 4718592 | tf_op jit(solution)/shard_map/all_to_all | solution.py:349
  98.8 1.8 %convert_reduce_fusion = f32[48,96]{1,0:T(8,128)S(1)} fusion(bf16[48,96,128]{2,1,0:T(8,128)(2,1)} %get-tuple-element.8.z_hbm), kind=kLoop, calls=%fused_computation.9 | loop fusion | flops 1175040 | bytes 1198080 | tf_op jit(solution)/shard_map/reduce_sum | solution.py:22
  100.6 31.6 %all-to-all-done.2.in_ref = bf16[128,72,128]{2,1,0:T(8,128)(2,1)S(1)} async-done(((bf16[128,72,128]{2,1,0:T(8,128)(2,1)}), bf16[128,72,128]{2,1,0:T(8,128)(2,1)S(1)}, u32[]{:S(2)}, u32[]{:S(2)}) %all-to-all-start.2) | async-done | bytes 2359328 | tf_op jit(solution)/shard_map/all_to_all | solution.py:349
  132.2 4.2 %tri.3 = bf16[128,40,128]{2,1,0:T(8,128)(2,1)} custom-call(bf16[128,72,128]{2,1,0:T(8,128)(2,1)S(1)} %all-to-all-done.2.in_ref), custom_call_target="tpu_custom_call" | custom-call | tf_op jit(solution)/shard_map/tri/pallas_call | solution.py:310
  136.4 0.0 copy-start.6
  136.4 4.5 %all-to-all-start.3 = ((bf16[128,40,128]{2,1,0:T(8,128)(2,1)}), bf16[128,40,128]{2,1,0:T(8,128)(2,1)S(1)}, u32[]{:S(2)}, u32[]{:S(2)}) async-start(bf16[128,40,128]{2,1,0:T(8,128)(2,1)} %tri.3), calls=%async_computation.3 | async-start | bytes 2621440 | tf_op jit(solution)/shard_map/all_to_all | solution.py:349
  141.0 1.6 fusion.10
  142.7 1.5 fusion.13
  144.2 2.2 %fusion.5 = f32[4608,128]{1,0:T(8,128)} fusion(bf16[4608,128]{1,0:T(8,128)(2,1)S(1)} %bitcast.23, bf16[2,128,640]{2,1,0:T(8,128)(2,1)S(1)} %copy-done), kind=kOutput, calls=%fused_computation.7 | convolution fusion | flops 152764416 | bytes 3571712 | tf_op jit(solution)/shard_map/dot_general | solution.py:343
  146.3 16.8 %all-to-all-done.3.prod = bf16[128,40,128]{2,1,0:T(8,128)(2,1)S(1)} async-done(((bf16[128,40,128]{2,1,0:T(8,128)(2,1)}), bf16[128,40,128]{2,1,0:T(8,128)(2,1)S(1)}, u32[]{:S(2)}, u32[]{:S(2)}) %all-to-all-start.3) | async-done | bytes 1310752 | tf_op jit(solution)/shard_map/all_to_all | solution.py:349
  163.1 5.0 %post.1 = bf16[48,96,128]{2,1,0:T(8,128)(2,1)} custom-call(bf16[128,40,128]{2,1,0:T(8,128)(2,1)S(1)} %all-to-all-done.3.prod, bf16[48,96,128]{2,1,0:T(8,128)(2,1)} %get-tuple-element.8.z_hbm, f32[48,96,128]{2,1,0:T(8,128)} %bitcast.21, f32[2,2,128]{2,1,0:T(2,128)S(1)} %copy-done.2, f32[2,2,128]{2,1,0:T(2,128)S(1)} %copy-done.3, ...), custom_call_target="tpu_custom_call" | custom-call | tf_op jit(solution)/shard_map/post/pallas_call | solution.py:310
  (8 shorter events, 0.0 us)
Async XLA Ops:
  7.8 44.8 %all-to-all-start = ((bf16[128,72,128]{2,1,0:T(8,128)(2,1)}), bf16[128,72,128]{2,1,0:T(8,128)(2,1)S(1)}, u32[]{:S(2)}, u32[]{:S(2)}) async-start(bf16[128,72,128]{2,1,0:T(8,128)(2,1)} %pre.1), calls=%async_computation | async-start | bytes 4718592 | tf_op jit(solution)/shard_map/all_to_all | solution.py:349
  56.8 7.4 %copy-start.2 = (f32[2,2,128]{2,1,0:T(2,128)S(1)}, f32[2,2,128]{2,1,0:T(2,128)}, u32[]{:S(2)}) copy-start(f32[2,2,128]{2,1,0:T(2,128)} %gains.3) | copy-start | bytes 6148
  56.8 7.4 %copy-start.3 = (f32[2,2,128]{2,1,0:T(2,128)S(1)}, f32[2,2,128]{2,1,0:T(2,128)}, u32[]{:S(2)}) copy-start(f32[2,2,128]{2,1,0:T(2,128)} %biases.3) | copy-start | bytes 6148
  56.8 7.4 %copy-start.5 = (bf16[48,96,128]{2,1,0:T(8,128)(2,1)S(1)}, bf16[48,96,128]{2,1,0:T(8,128)(2,1)}, u32[]{:S(2)}) copy-start(bf16[48,96,128]{2,1,0:T(8,128)(2,1)} %z_hbm.3) | copy-start | bytes 3538948
  56.8 26.7 %all-to-all-start.1 = ((bf16[128,40,128]{2,1,0:T(8,128)(2,1)}), bf16[128,40,128]{2,1,0:T(8,128)(2,1)S(1)}, u32[]{:S(2)}, u32[]{:S(2)}) async-start(bf16[128,40,128]{2,1,0:T(8,128)(2,1)} %tri.2), calls=%async_computation.1 | async-start | bytes 2621440 | tf_op jit(solution)/shard_map/all_to_all | solution.py:349
  61.4 4.3 %copy-start = (bf16[2,128,640]{2,1,0:T(8,128)(2,1)S(1)}, bf16[2,128,640]{2,1,0:T(8,128)(2,1)}, u32[]{:S(2)}) copy-start(bf16[2,128,640]{2,1,0:T(8,128)(2,1)} %w.1) | copy-start | bytes 983044
  65.7 17.9 %copy-start.1 = (bf16[2,128,128]{2,1,0:T(8,128)(2,1)S(1)}, bf16[2,128,128]{2,1,0:T(8,128)(2,1)}, u32[]{:S(2)}) copy-start(bf16[2,128,128]{2,1,0:T(8,128)(2,1)} %w_out.3) | copy-start | bytes 196612
  65.7 17.9 %copy-start.4 = (s32[8]{0:T(128)S(1)}, s32[8]{0:T(128)}, u32[]{:S(2)}) copy-start(s32[8]{0:T(128)} %chain.1) | copy-start | bytes 100
  94.4 37.8 %all-to-all-start.2 = ((bf16[128,72,128]{2,1,0:T(8,128)(2,1)}), bf16[128,72,128]{2,1,0:T(8,128)(2,1)S(1)}, u32[]{:S(2)}, u32[]{:S(2)}) async-start(bf16[128,72,128]{2,1,0:T(8,128)(2,1)} %get-tuple-element.7), calls=%async_computation.2 | async-start | bytes 4718592 | tf_op jit(solution)/shard_map/all_to_all | solution.py:349
  136.4 4.6 %copy-start.6 = (bf16[48,96,128]{2,1,0:T(8,128)(2,1)S(1)}, bf16[48,96,128]{2,1,0:T(8,128)(2,1)}, u32[]{:S(2)}) copy-start(bf16[48,96,128]{2,1,0:T(8,128)(2,1)} %get-tuple-element.8.z_hbm) | copy-start | bytes 3538948
  136.4 26.7 %all-to-all-start.3 = ((bf16[128,40,128]{2,1,0:T(8,128)(2,1)}), bf16[128,40,128]{2,1,0:T(8,128)(2,1)S(1)}, u32[]{:S(2)}, u32[]{:S(2)}) async-start(bf16[128,40,128]{2,1,0:T(8,128)(2,1)} %tri.3), calls=%async_computation.3 | async-start | bytes 2621440 | tf_op jit(solution)/shard_map/all_to_all | solution.py:349

commit v3 on v2

--- a/solution.py
+++ b/solution.py
@@ -12,8 +12,7 @@
 TR, TC = N // ROWS, N // COLS
 KHI, KLO = 3, 32
 NQ = 36
-SA, SP = 72, 40
-STORES = 8
+SA, SP = 24, 40
 BF, F32 = jnp.bfloat16, jnp.float32
 
 
@@ -111,30 +110,22 @@
     lax.fori_loop(0, ROWS // 2, finish, 0)
 
 
-def place(g):
-    h, part = g // 3, g % 3
-    tail = part == 2
-    row = jnp.where(tail, TR - 16, 4 * part)
-    step = jnp.where(tail, 4, 8)
-    factor_rows = [h * 24 + jnp.where(tail, 16 + 4 * side, 8 * side + 4 * part) for side in range(2)]
-    product_row = jnp.where(tail, 24 + 4 * h, 8 * h + 4 * part)
-    return h, row, step, factor_rows, product_row
-
-
-def copies(src, dst, sems, cuts):
-    return [pltpu.make_async_copy(src.at[k], dst.at[k], sems.at[n]) for n, k in enumerate(cuts)]
-
-
-def column_cuts():
-    return [(slice(None), pl.ds(h * KLO, KLO)) for h in range(KHI)]
-
-
-def wait_column(g, *lists):
-    for h in range(KHI):
-        @pl.when(g == 3 * h)
-        def _():
-            for some in lists:
-                some[h].wait()
+def place(part):
+    if part == 2:
+        return TR - 16, 4, (16, 20)
+    return 4 * part, 8, (4 * part, 8 + 4 * part)
+
+
+def product_row(part, h):
+    return 24 + 4 * h if part == 2 else 8 * h + 4 * part
+
+
+def column(ref, h):
+    return ref.at[:, pl.ds(pl.multiple_of(h * KLO, KLO), KLO)]
+
+
+def column_in(src, dst, sems, h):
+    return pltpu.make_async_copy(column(src, h), column(dst, h), sems.at[h])
 
 
 def load_chunk(z, row, step, h):
@@ -153,70 +144,82 @@
     live_rows = chain[row // 2] - TR * (row % 2)
     live_cols = chain[col]
     gain, bias = gains[u, 0:1, :], biases[u, 0:1, :]
-    w_t = [w[u, :, k * C:(k + 1) * C].T for k in range(4)]
+    columns = w[u, :, 0:4 * C].T
+    w_t = jnp.concatenate([
+        columns[(2 * side + k) * C + d:(2 * side + k) * C + d + 16]
+        for side in range(2) for d in range(0, C, 16) for k in range(2)
+    ], axis=0)
     lane = lax.broadcasted_iota(jnp.int32, (1, C), 1)
 
-    def project(chunks, h, first, step, factor_rows):
+    def project(chunks, h, part):
+        first, step, factor_rows = place(part)
         lane_row, lane_col = lane // KLO * step + first, lane % KLO + h * KLO
         for half in range(2):
             es = (2 * half, 2 * half + 1)
             normed = jnp.concatenate([norm_rows(chunks[e], gain, bias).astype(BF) for e in es], axis=0)
             mask = jnp.concatenate(
                 [((lane_row + e < live_rows) & (lane_col < live_cols)).astype(F32) for e in es], axis=1)
+            every = lax.dot_general(
+                w_t, normed, (((1,), (1,)), ((), ())), preferred_element_type=F32)
             for side in range(2):
-                value, gate = (
-                    lax.dot_general(
-                        w_t[2 * side + k], normed, (((1,), (1,)), ((), ())), preferred_element_type=F32)
-                    for k in range(2)
-                )
-                edges = mask * sigmoid(gate) * value
-                for n, e in enumerate(es):
-                    scr[pl.ds(factor_rows[side] + e, C, stride=SA), :] = edges[:, n * C:(n + 1) * C]
+                for d in range(0, C, 16):
+                    at = 2 * (side * C + d)
+                    value, gate = every[at:at + 16], every[at + 16:at + 32]
+                    edges = mask * sigmoid(gate) * value
+                    for n, e in enumerate(es):
+                        rows = pl.ds(d * SA + factor_rows[side] + e, 16, stride=SA)
+                        scr[rows, :] = edges[:, n * C:(n + 1) * C]
 
     return project
 
 
-def send_factors(scr, stage, out, sems):
-    per = C // STORES
-    outs = copies(stage, out, sems, [pl.ds(n * per, per) for n in range(STORES)])
-
+def factors_out(stage, out, sems, h):
+    return pltpu.make_async_copy(stage.at[h], out.at[:, pl.ds(pl.multiple_of(h * SA, SA), SA)], sems.at[h])
+
+
+def send_factors(scr, stage, out, sems, h):
     def cast(s, carry):
-        stage[s] = scr[pl.ds(pl.multiple_of(s * SA, 8), SA), :].astype(BF)
-        return carry
-
-    for n in range(STORES):
-        lax.fori_loop(n * per, (n + 1) * per, cast, 0, unroll=4)
-        outs[n].start()
-    return outs
+        stage[h, s] = scr[pl.ds(pl.multiple_of(s * SA, SA), SA), :].astype(BF)
+        return carry
+
+    lax.fori_loop(0, C, cast, 0, unroll=32)
+    factors_out(stage, out, sems, h).start()
+
+
+def each_column(step):
+    def one(h, carry):
+        step(h)
+        return carry
+
+    lax.fori_loop(0, KHI, one, 0)
 
 
 def pre_kernel(chain_hbm, z_hbm, w_hbm, gain_hbm, bias_hbm, out_hbm,
                chain, z, w, gains, biases, scr, stage, in_sems, z_sems, out_sems):
     small = [pltpu.make_async_copy(a, b, in_sems.at[n]) for n, (a, b) in enumerate(
         ((chain_hbm, chain), (w_hbm, w), (gain_hbm, gains), (bias_hbm, biases)))]
-    z_in = copies(z_hbm, z, z_sems, column_cuts())
-    for one in small + z_in:
+    for one in small + [column_in(z_hbm, z, z_sems, h) for h in range(KHI)]:
         one.start()
     for one in small:
         one.wait()
     project = projector(chain, w, gains, biases, scr, 0)
 
-    def step(g, carry):
-        wait_column(g, z_in)
-        h, row, gap, factor_rows, _ = place(g)
-        project([load_chunk(z, row + e, gap, h) for e in range(4)], h, row, gap, factor_rows)
-        return carry
-
-    lax.fori_loop(0, 9, step, 0)
-    for one in send_factors(scr, stage, out_hbm, out_sems):
-        one.wait()
+    def step(h):
+        column_in(z_hbm, z, z_sems, h).wait()
+        for part in range(3):
+            row, gap = place(part)[:2]
+            project([load_chunk(z, row + e, gap, h) for e in range(4)], h, part)
+        send_factors(scr, stage, out_hbm, out_sems, h)
+
+    each_column(step)
+    for h in range(KHI):
+        factors_out(stage, out_hbm, out_sems, h).wait()
 
 
 def post_parts(prod, z_hbm, gate_hbm, gains, biases, w_out, z, gate, wide, z_sems, gate_sems, u):
-    z_in = copies(z_hbm, z, z_sems, column_cuts())
-    gate_in = copies(gate_hbm, gate, gate_sems, column_cuts())
-    for one in z_in + gate_in:
-        one.start()
+    for h in range(KHI):
+        column_in(z_hbm, z, z_sems, h).start()
+        column_in(gate_hbm, gate, gate_sems, h).start()
     gain = jnp.broadcast_to(gains[u, 1:2, :], (C, C)).T
     bias = jnp.broadcast_to(biases[u, 1:2, :], (C, C)).T
 
@@ -224,11 +227,15 @@
         wide[pl.ds(pl.multiple_of(s * SP, 8), SP), :] = prod[s].astype(F32)
         return carry
 
-    lax.fori_loop(0, C, widen, 0, unroll=4)
-
-    def chunk(g, e):
-        h, row, gap, _, product_row = place(g)
-        x = wide[pl.ds(product_row + e, C, stride=SP), :]
+    lax.fori_loop(0, C, widen, 0, unroll=8)
+
+    def ready(h):
+        column_in(z_hbm, z, z_sems, h).wait()
+        column_in(gate_hbm, gate, gate_sems, h).wait()
+
+    def chunk(h, part, e):
+        row, gap = place(part)[:2]
+        x = wide[pl.ds(product_row(part, h) + e, C, stride=SP), :]
         mean = jnp.mean(x, axis=0, keepdims=True)
         centred = x - mean
         var = jnp.mean(centred * centred, axis=0, keepdims=True)
@@ -238,54 +245,48 @@
         old = load_chunk(z, row + e, gap, h).astype(F32)
         return (old + load_chunk(gate, row + e, gap, h) * mixed).astype(BF)
 
-    return z_in, gate_in, chunk
+    return ready, chunk
 
 
 def mid_kernel(chain, prod, z_hbm, gate_hbm, w, gains, biases, w_out, z_out_hbm, out_hbm,
                z, gate, wide, z_out, scr, stage, z_sems, gate_sems, zo_sems, out_sems):
-    z_in, gate_in, chunk = post_parts(
+    ready, chunk = post_parts(
         prod, z_hbm, gate_hbm, gains, biases, w_out, z, gate, wide, z_sems, gate_sems, 0)
     project = projector(chain, w, gains, biases, scr, 1)
-    z_done = copies(z_out, z_out_hbm, zo_sems, column_cuts())
-
-    def step(g, carry):
-        wait_column(g, z_in, gate_in)
-        h, row, gap, factor_rows, _ = place(g)
-        new = [chunk(g, e) for e in range(4)]
-        for e in range(4):
-            store_chunk(z_out, row + e, gap, h, new[e])
-        project(new, h, row, gap, factor_rows)
-        for k in range(KHI):
-            @pl.when(g == 3 * k + 2)
-            def _():
-                z_done[k].start()
-        return carry
-
-    lax.fori_loop(0, 9, step, 0)
-    for one in send_factors(scr, stage, out_hbm, out_sems) + z_done:
-        one.wait()
+
+    def step(h):
+        ready(h)
+        for part in range(3):
+            row, gap = place(part)[:2]
+            new = [chunk(h, part, e) for e in range(4)]
+            for e in range(4):
+                store_chunk(z_out, row + e, gap, h, new[e])
+            project(new, h, part)
+        column_in(z_out, z_out_hbm, zo_sems, h).start()
+        send_factors(scr, stage, out_hbm, out_sems, h)
+
+    each_column(step)
+    for h in range(KHI):
+        column_in(z_out, z_out_hbm, zo_sems, h).wait()
+        factors_out(stage, out_hbm, out_sems, h).wait()
 
 
 def post_kernel(prod, z_hbm, gate_hbm, gains, biases, w_out, z_out_hbm,
                 z, gate, wide, z_out, z_sems, gate_sems, zo_sems):
-    z_in, gate_in, chunk = post_parts(
+    ready, chunk = post_parts(
         prod, z_hbm, gate_hbm, gains, biases, w_out, z, gate, wide, z_sems, gate_sems, 1)
-    z_done = copies(z_out, z_out_hbm, zo_sems, column_cuts())
-
-    def step(g, carry):
-        wait_column(g, z_in, gate_in)
-        h, row, gap, _, _ = place(g)
-        for e in range(4):
-            store_chunk(z_out, row + e, gap, h, chunk(g, e))
-        for k in range(KHI):
-            @pl.when(g == 3 * k + 2)
-            def _():
-                z_done[k].start()
-        return carry
-
-    lax.fori_loop(0, 9, step, 0)
-    for one in z_done:
-        one.wait()
+
+    def step(h):
+        ready(h)
+        for part in range(3):
+            row, gap = place(part)[:2]
+            for e in range(4):
+                store_chunk(z_out, row + e, gap, h, chunk(h, part, e))
+        column_in(z_out, z_out_hbm, zo_sems, h).start()
+
+    each_column(step)
+    for h in range(KHI):
+        column_in(z_out, z_out_hbm, zo_sems, h).wait()
 
 
 HBM = pl.BlockSpec(memory_space=pltpu.HBM)
@@ -318,11 +319,11 @@
 
 def kernels():
     V = pltpu.VMEM
-    send = [V((C * SA, C), F32), V(*FACTORS)]
+    send = [V((C * SA, C), F32), V((KHI, C, SA, C), BF)]
     pre = call(
         pre_kernel, "pre", [FACTORS],
         [pltpu.SMEM((8,), jnp.int32), V(*STATE), V((2, C, 5 * C), BF), V((2, 2, C), F32), V((2, 2, C), F32)] + send,
-        [4, KHI, STORES], 20, [HBM] * 5)
+        [4, KHI, KHI], 20, [HBM] * 5)
     tri = [
         call(
             functools.partial(tri_kernel, incoming=u == 1), "tri", [PRODUCTS],
@@ -331,7 +332,7 @@
     ]
     take = [V(*STATE), V(STATE[0], F32), V((C * SP, C), F32), V(*STATE)]
     mid = call(
-        mid_kernel, "mid", [STATE, FACTORS], take + send, [KHI, KHI, KHI, STORES], 26,
+        mid_kernel, "mid", [STATE, FACTORS], take + send, [KHI, KHI, KHI, KHI], 26,
         [SMEM, VMEM] + [HBM] * 2 + [VMEM] * 4)
     post = call(
         post_kernel, "post", [STATE], take, [KHI, KHI, KHI], 16, [VMEM] + [HBM] * 2 + [VMEM] * 3)

time: 169 us -> 163 us (0.964)
  Pallas kernels: 32 us -> 26.3 us
    pallas_call x5, Pallas kernels: 32 us -> 26.3 us  [placed(): run(*(pltpu.with_memory_space_constraint(a, s.memory_space) if s is HBM o...]
where the time goes in v3:
time: 163 us
  waiting for transfers between devices  95.6 us (59%)
  Pallas kernels  26.3 us (16%)
  starting transfers between devices  25 us (15%)
  other arithmetic  10.9 us (7%)
  matrix products  4.38 us (3%)
    all_to_all x4, waiting for transfers between devices, exchange(): return lax.all_to_all(blocks, ('row', 'col'), 0, 0, tiled=True)  95.6 us
    pallas_call x5, Pallas kernels, placed(): run(*(pltpu.with_memory_space_constraint(a, s.memory_space) if s is HBM o...  26.3 us
    all_to_all x4, starting transfers between devices, exchange(): return lax.all_to_all(blocks, ('row', 'col'), 0, 0, tiled=True)  25 us
    reduce_sum x2, other arithmetic, norm_rows(): var = jnp.mean(centred * centred, axis=1, keepdims=True)  4.39 us
    dot_general x2, matrix products, output_gate(): jnp.dot(normed, w_in[u, :, 4 * C:], preferred_element_type=F32)  4.38 us
    reduce_sum x2, other arithmetic, norm_rows(): mean = jnp.mean(wide, axis=1, keepdims=True)  3.52 us
  transfers between devices with their start and end apart: 4, of which 4 were waited for; matrix products, arithmetic and copies ran while one was open for 9% of the time, Pallas kernels for 0%

profile of v3, /device:TPU:1, one launch (start us, length us, event | category | flops | bytes accessed | tf_op | source)
XLA Modules:
  0.0 162.6 jit_solution(13542614718926086428)
XLA Ops:
  0.0 5.3 %pre.1 = bf16[128,72,128]{2,1,0:T(8,128)(2,1)} custom-call(s32[8]{0:T(128)} %chain.1, bf16[48,96,128]{2,1,0:T(8,128)(2,1)} %z_hbm.3, bf16[2,128,640]{2,1,0:T(8,128)(2,1)} %w.1, f32[2,2,128]{2,1,0:T(2,128)} %gains.3, f32[2,2,128]{2,1,0:T(2,128)} %biases.3), custom_call_target="tpu_custom_call" | custom-call | tf_op jit(solution)/shard_map/pre/pallas_call | solution.py:311
  5.3 11.5 %all-to-all-start = ((bf16[128,72,128]{2,1,0:T(8,128)(2,1)}), bf16[128,72,128]{2,1,0:T(8,128)(2,1)S(1)}, u32[]{:S(2)}, u32[]{:S(2)}) async-start(bf16[128,72,128]{2,1,0:T(8,128)(2,1)} %pre.1), calls=%async_computation | async-start | bytes 4718592 | tf_op jit(solution)/shard_map/all_to_all | solution.py:350
  16.8 1.8 %convert_reduce_fusion.1 = f32[48,96]{1,0:T(8,128)S(1)} fusion(bf16[48,96,128]{2,1,0:T(8,128)(2,1)} %z_hbm.3), kind=kLoop, calls=%fused_computation.11 | loop fusion | flops 1175040 | bytes 1198080 | tf_op jit(solution)/shard_map/reduce_sum | solution.py:21
  18.6 31.5 %all-to-all-done.in_ref = bf16[128,72,128]{2,1,0:T(8,128)(2,1)S(1)} async-done(((bf16[128,72,128]{2,1,0:T(8,128)(2,1)}), bf16[128,72,128]{2,1,0:T(8,128)(2,1)S(1)}, u32[]{:S(2)}, u32[]{:S(2)}) %all-to-all-start) | async-done | bytes 2359328 | tf_op jit(solution)/shard_map/all_to_all | solution.py:350
  50.1 4.2 %tri.2 = bf16[128,40,128]{2,1,0:T(8,128)(2,1)} custom-call(bf16[128,72,128]{2,1,0:T(8,128)(2,1)S(1)} %all-to-all-done.in_ref), custom_call_target="tpu_custom_call" | custom-call | tf_op jit(solution)/shard_map/tri/pallas_call | solution.py:311
  54.3 0.0 copy-start.2
  54.3 0.0 copy-start.3
  54.3 0.0 copy-start.5
  54.4 4.5 %all-to-all-start.1 = ((bf16[128,40,128]{2,1,0:T(8,128)(2,1)}), bf16[128,40,128]{2,1,0:T(8,128)(2,1)S(1)}, u32[]{:S(2)}, u32[]{:S(2)}) async-start(bf16[128,40,128]{2,1,0:T(8,128)(2,1)} %tri.2), calls=%async_computation.1 | async-start | bytes 2621440 | tf_op jit(solution)/shard_map/all_to_all | solution.py:350
  58.9 0.0 copy-start
  58.9 2.7 %fusion.14 = f32[48,96]{1,0:T(8,128)S(1)} fusion(bf16[48,96,128]{2,1,0:T(8,128)(2,1)} %z_hbm.3, f32[48,96]{1,0:T(8,128)S(1)} %broadcast_multiply_fusion.1), kind=kLoop, calls=%fused_computation.20 | loop fusion | flops 2354688 | bytes 1216512 | tf_op jit(solution)/shard_map/reduce_sum | solution.py:23
  61.7 0.0 copy-done.2
  61.7 0.0 copy-done.3
  61.7 0.0 copy-done.5
  61.7 1.5 fusion.17
  63.2 0.0 copy-done
  63.2 0.0 copy-start.1
  63.2 0.0 copy-start.4
  63.2 2.2 %fusion.4 = f32[4608,128]{1,0:T(8,128)} fusion(bf16[4608,128]{1,0:T(8,128)(2,1)S(1)} %bitcast.22, bf16[2,128,640]{2,1,0:T(8,128)(2,1)S(1)} %copy-done), kind=kOutput, calls=%fused_computation.6 | convolution fusion | flops 152764416 | bytes 3571712 | tf_op jit(solution)/shard_map/dot_general | solution.py:344
  65.4 15.6 %all-to-all-done.1.prod = bf16[128,40,128]{2,1,0:T(8,128)(2,1)S(1)} async-done(((bf16[128,40,128]{2,1,0:T(8,128)(2,1)}), bf16[128,40,128]{2,1,0:T(8,128)(2,1)S(1)}, u32[]{:S(2)}, u32[]{:S(2)}) %all-to-all-start.1) | async-done | bytes 1310752 | tf_op jit(solution)/shard_map/all_to_all | solution.py:350
  81.1 8.9 %mid.1 = (bf16[48,96,128]{2,1,0:T(8,128)(2,1)}, bf16[128,72,128]{2,1,0:T(8,128)(2,1)}) custom-call(s32[8]{0:T(128)S(1)} %copy-done.4, bf16[128,40,128]{2,1,0:T(8,128)(2,1)S(1)} %all-to-all-done.1.prod, bf16[48,96,128]{2,1,0:T(8,128)(2,1)} %z_hbm.3, f32[48,96,128]{2,1,0:T(8,128)} %bitcast.20, bf16[2,128,640]{2,1,0:T(8,128)(2,1)S(1)} %copy-done, ...), custom_call_target="tpu_custom_call" | custom-call | tf_op jit(solution)/shard_map/mid/pallas_call | solution.py:311
  90.0 4.4 %all-to-all-start.2 = ((bf16[128,72,128]{2,1,0:T(8,128)(2,1)}), bf16[128,72,128]{2,1,0:T(8,128)(2,1)S(1)}, u32[]{:S(2)}, u32[]{:S(2)}) async-start(bf16[128,72,128]{2,1,0:T(8,128)(2,1)} %get-tuple-element.7), calls=%async_computation.2 | async-start | bytes 4718592 | tf_op jit(solution)/shard_map/all_to_all | solution.py:350
  94.4 1.8 %convert_reduce_fusion = f32[48,96]{1,0:T(8,128)S(1)} fusion(bf16[48,96,128]{2,1,0:T(8,128)(2,1)} %get-tuple-element.8.z_hbm), kind=kLoop, calls=%fused_computation.9 | loop fusion | flops 1175040 | bytes 1198080 | tf_op jit(solution)/shard_map/reduce_sum | solution.py:21
  96.1 31.6 %all-to-all-done.2.in_ref = bf16[128,72,128]{2,1,0:T(8,128)(2,1)S(1)} async-done(((bf16[128,72,128]{2,1,0:T(8,128)(2,1)}), bf16[128,72,128]{2,1,0:T(8,128)(2,1)S(1)}, u32[]{:S(2)}, u32[]{:S(2)}) %all-to-all-start.2) | async-done | bytes 2359328 | tf_op jit(solution)/shard_map/all_to_all | solution.py:350
  127.8 4.2 %tri.3 = bf16[128,40,128]{2,1,0:T(8,128)(2,1)} custom-call(bf16[128,72,128]{2,1,0:T(8,128)(2,1)S(1)} %all-to-all-done.2.in_ref), custom_call_target="tpu_custom_call" | custom-call | tf_op jit(solution)/shard_map/tri/pallas_call | solution.py:311
  132.0 4.6 %all-to-all-start.3 = ((bf16[128,40,128]{2,1,0:T(8,128)(2,1)}), bf16[128,40,128]{2,1,0:T(8,128)(2,1)S(1)}, u32[]{:S(2)}, u32[]{:S(2)}) async-start(bf16[128,40,128]{2,1,0:T(8,128)(2,1)} %tri.3), calls=%async_computation.3 | async-start | bytes 2621440 | tf_op jit(solution)/shard_map/all_to_all | solution.py:350
  136.6 0.0 copy-done.6
  136.6 1.6 %fusion.10 = f32[48,96]{1,0:T(8,128)S(1)} fusion(bf16[48,96,128]{2,1,0:T(8,128)(2,1)S(1)} %copy-done.6, f32[48,96]{1,0:T(8,128)S(1)} %broadcast_multiply_fusion), kind=kLoop, calls=%fused_computation.16 | loop fusion | flops 2354688 | bytes 1216512 | tf_op jit(solution)/shard_map/reduce_sum | solution.py:23
  138.3 1.5 fusion.13
  139.7 2.2 %fusion.5 = f32[4608,128]{1,0:T(8,128)} fusion(bf16[4608,128]{1,0:T(8,128)(2,1)S(1)} %bitcast.23, bf16[2,128,640]{2,1,0:T(8,128)(2,1)S(1)} %copy-done), kind=kOutput, calls=%fused_computation.7 | convolution fusion | flops 152764416 | bytes 3571712 | tf_op jit(solution)/shard_map/dot_general | solution.py:344
  141.9 16.8 %all-to-all-done.3.prod = bf16[128,40,128]{2,1,0:T(8,128)(2,1)S(1)} async-done(((bf16[128,40,128]{2,1,0:T(8,128)(2,1)}), bf16[128,40,128]{2,1,0:T(8,128)(2,1)S(1)}, u32[]{:S(2)}, u32[]{:S(2)}) %all-to-all-start.3) | async-done | bytes 1310752 | tf_op jit(solution)/shard_map/all_to_all | solution.py:350
  158.7 3.7 %post.1 = bf16[48,96,128]{2,1,0:T(8,128)(2,1)} custom-call(bf16[128,40,128]{2,1,0:T(8,128)(2,1)S(1)} %all-to-all-done.3.prod, bf16[48,96,128]{2,1,0:T(8,128)(2,1)} %get-tuple-element.8.z_hbm, f32[48,96,128]{2,1,0:T(8,128)} %bitcast.21, f32[2,2,128]{2,1,0:T(2,128)S(1)} %copy-done.2, f32[2,2,128]{2,1,0:T(2,128)S(1)} %copy-done.3, ...), custom_call_target="tpu_custom_call" | custom-call | tf_op jit(solution)/shard_map/post/pallas_call | solution.py:311
  (8 shorter events, 0.0 us)
Async XLA Ops:
  5.3 44.8 %all-to-all-start = ((bf16[128,72,128]{2,1,0:T(8,128)(2,1)}), bf16[128,72,128]{2,1,0:T(8,128)(2,1)S(1)}, u32[]{:S(2)}, u32[]{:S(2)}) async-start(bf16[128,72,128]{2,1,0:T(8,128)(2,1)} %pre.1), calls=%async_computation | async-start | bytes 4718592 | tf_op jit(solution)/shard_map/all_to_all | solution.py:350
  54.3 7.4 %copy-start.2 = (f32[2,2,128]{2,1,0:T(2,128)S(1)}, f32[2,2,128]{2,1,0:T(2,128)}, u32[]{:S(2)}) copy-start(f32[2,2,128]{2,1,0:T(2,128)} %gains.3) | copy-start | bytes 6148
  54.3 7.4 %copy-start.3 = (f32[2,2,128]{2,1,0:T(2,128)S(1)}, f32[2,2,128]{2,1,0:T(2,128)}, u32[]{:S(2)}) copy-start(f32[2,2,128]{2,1,0:T(2,128)} %biases.3) | copy-start | bytes 6148
  54.3 7.4 %copy-start.5 = (bf16[48,96,128]{2,1,0:T(8,128)(2,1)S(1)}, bf16[48,96,128]{2,1,0:T(8,128)(2,1)}, u32[]{:S(2)}) copy-start(bf16[48,96,128]{2,1,0:T(8,128)(2,1)} %z_hbm.3) | copy-start | bytes 3538948
  54.4 26.7 %all-to-all-start.1 = ((bf16[128,40,128]{2,1,0:T(8,128)(2,1)}), bf16[128,40,128]{2,1,0:T(8,128)(2,1)S(1)}, u32[]{:S(2)}, u32[]{:S(2)}) async-start(bf16[128,40,128]{2,1,0:T(8,128)(2,1)} %tri.2), calls=%async_computation.1 | async-start | bytes 2621440 | tf_op jit(solution)/shard_map/all_to_all | solution.py:350
  58.9 4.3 %copy-start = (bf16[2,128,640]{2,1,0:T(8,128)(2,1)S(1)}, bf16[2,128,640]{2,1,0:T(8,128)(2,1)}, u32[]{:S(2)}) copy-start(bf16[2,128,640]{2,1,0:T(8,128)(2,1)} %w.1) | copy-start | bytes 983044
  63.2 17.9 %copy-start.1 = (bf16[2,128,128]{2,1,0:T(8,128)(2,1)S(1)}, bf16[2,128,128]{2,1,0:T(8,128)(2,1)}, u32[]{:S(2)}) copy-start(bf16[2,128,128]{2,1,0:T(8,128)(2,1)} %w_out.3) | copy-start | bytes 196612
  63.2 17.9 %copy-start.4 = (s32[8]{0:T(128)S(1)}, s32[8]{0:T(128)}, u32[]{:S(2)}) copy-start(s32[8]{0:T(128)} %chain.1) | copy-start | bytes 100
  90.0 37.8 %all-to-all-start.2 = ((bf16[128,72,128]{2,1,0:T(8,128)(2,1)}), bf16[128,72,128]{2,1,0:T(8,128)(2,1)S(1)}, u32[]{:S(2)}, u32[]{:S(2)}) async-start(bf16[128,72,128]{2,1,0:T(8,128)(2,1)} %get-tuple-element.7), calls=%async_computation.2 | async-start | bytes 4718592 | tf_op jit(solution)/shard_map/all_to_all | solution.py:350
  132.0 4.6 %copy-start.6 = (bf16[48,96,128]{2,1,0:T(8,128)(2,1)S(1)}, bf16[48,96,128]{2,1,0:T(8,128)(2,1)}, u32[]{:S(2)}) copy-start(bf16[48,96,128]{2,1,0:T(8,128)(2,1)} %get-tuple-element.8.z_hbm) | copy-start | bytes 3538948
  132.0 26.7 %all-to-all-start.3 = ((bf16[128,40,128]{2,1,0:T(8,128)(2,1)}), bf16[128,40,128]{2,1,0:T(8,128)(2,1)S(1)}, u32[]{:S(2)}, u32[]{:S(2)}) async-start(bf16[128,40,128]{2,1,0:T(8,128)(2,1)} %tri.3), calls=%async_computation.3 | async-start | bytes 2621440 | tf_op jit(solution)/shard_map/all_to_all | solution.py:350

commit v4 on v3

--- a/solution.py
+++ b/solution.py
@@ -61,7 +61,7 @@
             mrb[rows, lanes] = jnp.concatenate(right, axis=0).astype(BF)
         return carry
 
-    lax.fori_loop(0, ROWS, gather, 0, unroll=2)
+    lax.fori_loop(0, ROWS, gather, 0, unroll=4)
     for m in range(2):
         cut = slice(m * 384, (m + 1) * 384)
         if incoming:
@@ -101,7 +101,7 @@
         copy_out(t).start()
         return carry
 
-    lax.fori_loop(0, ROWS // 2, scatter, 0)
+    lax.fori_loop(0, ROWS // 2, scatter, 0, unroll=2)
 
     def finish(r, carry):
         copy_out(r).wait()
@@ -144,7 +144,7 @@
     live_rows = chain[row // 2] - TR * (row % 2)
     live_cols = chain[col]
     gain, bias = gains[u, 0:1, :], biases[u, 0:1, :]
-    columns = w[u, :, 0:4 * C].T
+    columns = (w[u, :, 0:4 * C].astype(F32) * 0.5).T.astype(BF)
     w_t = jnp.concatenate([
         columns[(2 * side + k) * C + d:(2 * side + k) * C + d + 16]
         for side in range(2) for d in range(0, C, 16) for k in range(2)
@@ -165,7 +165,7 @@
                 for d in range(0, C, 16):
                     at = 2 * (side * C + d)
                     value, gate = every[at:at + 16], every[at + 16:at + 32]
-                    edges = mask * sigmoid(gate) * value
+                    edges = mask * (value * jnp.tanh(gate) + value)
                     for n, e in enumerate(es):
                         rows = pl.ds(d * SA + factor_rows[side] + e, 16, stride=SA)
                         scr[rows, :] = edges[:, n * C:(n + 1) * C]
@@ -227,7 +227,7 @@
         wide[pl.ds(pl.multiple_of(s * SP, 8), SP), :] = prod[s].astype(F32)
         return carry
 
-    lax.fori_loop(0, C, widen, 0, unroll=8)
+    lax.fori_loop(0, C, widen, 0, unroll=32)
 
     def ready(h):
         column_in(z_hbm, z, z_sems, h).wait()
@@ -254,17 +254,21 @@
         prod, z_hbm, gate_hbm, gains, biases, w_out, z, gate, wide, z_sems, gate_sems, 0)
     project = projector(chain, w, gains, biases, scr, 1)
 
-    def step(h):
+    def update(h):
         ready(h)
         for part in range(3):
             row, gap = place(part)[:2]
-            new = [chunk(h, part, e) for e in range(4)]
             for e in range(4):
-                store_chunk(z_out, row + e, gap, h, new[e])
-            project(new, h, part)
+                store_chunk(z_out, row + e, gap, h, chunk(h, part, e))
         column_in(z_out, z_out_hbm, zo_sems, h).start()
+
+    def step(h):
+        for part in range(3):
+            row, gap = place(part)[:2]
+            project([load_chunk(z_out, row + e, gap, h) for e in range(4)], h, part)
         send_factors(scr, stage, out_hbm, out_sems, h)
 
+    each_column(update)
     each_column(step)
     for h in range(KHI):
         column_in(z_out, z_out_hbm, zo_sems, h).wait()

time: 163 us -> 161 us (0.988)
  Pallas kernels: 26.3 us -> 24 us
    pallas_call x5, Pallas kernels: 26.3 us -> 24 us  [placed(): run(*(pltpu.with_memory_space_constraint(a, s.memory_space) if s is HBM o...]
  transfers between devices with their start and end apart: 4 -> 4, of which waited for: 4 -> 4; matrix products, arithmetic and copies ran while one was open for 9% -> 10% of each run, Pallas kernels for 0% -> 0%
where the time goes in v4:
time: 161 us; the launch traced here: 160 us
  waiting for transfers between devices  95.6 us (59%)
  starting transfers between devices  25 us (16%)
  Pallas kernels  24 us (15%)
  other arithmetic  10.9 us (7%)
  matrix products  4.39 us (3%)
    all_to_all x4, waiting for transfers between devices, exchange(): return lax.all_to_all(blocks, ('row', 'col'), 0, 0, tiled=True)  95.6 us
    all_to_all x4, starting transfers between devices, exchange(): return lax.all_to_all(blocks, ('row', 'col'), 0, 0, tiled=True)  25 us
    pallas_call x5, Pallas kernels, placed(): run(*(pltpu.with_memory_space_constraint(a, s.memory_space) if s is HBM o...  24 us
    reduce_sum x2, other arithmetic, norm_rows(): var = jnp.mean(centred * centred, axis=1, keepdims=True)  4.39 us
    dot_general x2, matrix products, output_gate(): jnp.dot(normed, w_in[u, :, 4 * C:], preferred_element_type=F32)  4.39 us
    reduce_sum x2, other arithmetic, norm_rows(): mean = jnp.mean(wide, axis=1, keepdims=True)  3.52 us
  transfers between devices with their start and end apart: 4, of which 4 were waited for; matrix products, arithmetic and copies ran while one was open for 10% of the time, Pallas kernels for 0%

profile of v4, /device:TPU:1, one launch (start us, length us, event | category | flops | bytes accessed | tf_op | source)
XLA Modules:
  0.0 160.3 jit_solution(738883860759244105)
XLA Ops:
  0.0 5.1 %pre.1 = bf16[128,72,128]{2,1,0:T(8,128)(2,1)} custom-call(s32[8]{0:T(128)} %chain.1, bf16[48,96,128]{2,1,0:T(8,128)(2,1)} %z_hbm.3, bf16[2,128,640]{2,1,0:T(8,128)(2,1)} %w.1, f32[2,2,128]{2,1,0:T(2,128)} %gains.3, f32[2,2,128]{2,1,0:T(2,128)} %biases.3), custom_call_target="tpu_custom_call" | custom-call | tf_op jit(solution)/shard_map/pre/pallas_call | solution.py:315
  5.1 11.5 %all-to-all-start = ((bf16[128,72,128]{2,1,0:T(8,128)(2,1)}), bf16[128,72,128]{2,1,0:T(8,128)(2,1)S(1)}, u32[]{:S(2)}, u32[]{:S(2)}) async-start(bf16[128,72,128]{2,1,0:T(8,128)(2,1)} %pre.1), calls=%async_computation | async-start | bytes 4718592 | tf_op jit(solution)/shard_map/all_to_all | solution.py:354
  16.6 1.8 %convert_reduce_fusion.1 = f32[48,96]{1,0:T(8,128)S(1)} fusion(bf16[48,96,128]{2,1,0:T(8,128)(2,1)} %z_hbm.3), kind=kLoop, calls=%fused_computation.11 | loop fusion | flops 1175040 | bytes 1198080 | tf_op jit(solution)/shard_map/reduce_sum | solution.py:21
  18.4 31.5 %all-to-all-done.in_ref = bf16[128,72,128]{2,1,0:T(8,128)(2,1)S(1)} async-done(((bf16[128,72,128]{2,1,0:T(8,128)(2,1)}), bf16[128,72,128]{2,1,0:T(8,128)(2,1)S(1)}, u32[]{:S(2)}, u32[]{:S(2)}) %all-to-all-start) | async-done | bytes 2359328 | tf_op jit(solution)/shard_map/all_to_all | solution.py:354
  49.9 3.8 %tri.2 = bf16[128,40,128]{2,1,0:T(8,128)(2,1)} custom-call(bf16[128,72,128]{2,1,0:T(8,128)(2,1)S(1)} %all-to-all-done.in_ref), custom_call_target="tpu_custom_call" | custom-call | tf_op jit(solution)/shard_map/tri/pallas_call | solution.py:315
  53.7 0.0 copy-start.2
  53.7 0.0 copy-start.3
  53.7 0.0 copy-start.5
  53.7 4.5 %all-to-all-start.1 = ((bf16[128,40,128]{2,1,0:T(8,128)(2,1)}), bf16[128,40,128]{2,1,0:T(8,128)(2,1)S(1)}, u32[]{:S(2)}, u32[]{:S(2)}) async-start(bf16[128,40,128]{2,1,0:T(8,128)(2,1)} %tri.2), calls=%async_computation.1 | async-start | bytes 2621440 | tf_op jit(solution)/shard_map/all_to_all | solution.py:354
  58.3 0.0 copy-start
  58.3 2.7 %fusion.14 = f32[48,96]{1,0:T(8,128)S(1)} fusion(bf16[48,96,128]{2,1,0:T(8,128)(2,1)} %z_hbm.3, f32[48,96]{1,0:T(8,128)S(1)} %broadcast_multiply_fusion.1), kind=kLoop, calls=%fused_computation.20 | loop fusion | flops 2354688 | bytes 1216512 | tf_op jit(solution)/shard_map/reduce_sum | solution.py:23
  61.1 0.0 copy-done.2
  61.1 0.0 copy-done.3
  61.1 0.0 copy-done.5
  61.1 1.5 fusion.17
  62.6 0.0 copy-done
  62.6 0.0 copy-start.1
  62.6 0.0 copy-start.4
  62.6 2.2 %fusion.4 = f32[4608,128]{1,0:T(8,128)} fusion(bf16[4608,128]{1,0:T(8,128)(2,1)S(1)} %bitcast.22, bf16[2,128,640]{2,1,0:T(8,128)(2,1)S(1)} %copy-done), kind=kOutput, calls=%fused_computation.6 | convolution fusion | flops 152764416 | bytes 3571712 | tf_op jit(solution)/shard_map/dot_general | solution.py:348
  64.8 15.6 %all-to-all-done.1.prod = bf16[128,40,128]{2,1,0:T(8,128)(2,1)S(1)} async-done(((bf16[128,40,128]{2,1,0:T(8,128)(2,1)}), bf16[128,40,128]{2,1,0:T(8,128)(2,1)S(1)}, u32[]{:S(2)}, u32[]{:S(2)}) %all-to-all-start.1) | async-done | bytes 1310752 | tf_op jit(solution)/shard_map/all_to_all | solution.py:354
  80.5 0.0 copy-done.4
  80.5 7.5 %mid.1 = (bf16[48,96,128]{2,1,0:T(8,128)(2,1)}, bf16[128,72,128]{2,1,0:T(8,128)(2,1)}) custom-call(s32[8]{0:T(128)S(1)} %copy-done.4, bf16[128,40,128]{2,1,0:T(8,128)(2,1)S(1)} %all-to-all-done.1.prod, bf16[48,96,128]{2,1,0:T(8,128)(2,1)} %z_hbm.3, f32[48,96,128]{2,1,0:T(8,128)} %bitcast.20, bf16[2,128,640]{2,1,0:T(8,128)(2,1)S(1)} %copy-done, ...), custom_call_target="tpu_custom_call" | custom-call | tf_op jit(solution)/shard_map/mid/pallas_call | solution.py:315
  88.0 4.4 %all-to-all-start.2 = ((bf16[128,72,128]{2,1,0:T(8,128)(2,1)}), bf16[128,72,128]{2,1,0:T(8,128)(2,1)S(1)}, u32[]{:S(2)}, u32[]{:S(2)}) async-start(bf16[128,72,128]{2,1,0:T(8,128)(2,1)} %get-tuple-element.7), calls=%async_computation.2 | async-start | bytes 4718592 | tf_op jit(solution)/shard_map/all_to_all | solution.py:354
  92.4 1.8 %convert_reduce_fusion = f32[48,96]{1,0:T(8,128)S(1)} fusion(bf16[48,96,128]{2,1,0:T(8,128)(2,1)} %get-tuple-element.8.z_hbm), kind=kLoop, calls=%fused_computation.9 | loop fusion | flops 1175040 | bytes 1198080 | tf_op jit(solution)/shard_map/reduce_sum | solution.py:21
  94.2 31.6 %all-to-all-done.2.in_ref = bf16[128,72,128]{2,1,0:T(8,128)(2,1)S(1)} async-done(((bf16[128,72,128]{2,1,0:T(8,128)(2,1)}), bf16[128,72,128]{2,1,0:T(8,128)(2,1)S(1)}, u32[]{:S(2)}, u32[]{:S(2)}) %all-to-all-start.2) | async-done | bytes 2359328 | tf_op jit(solution)/shard_map/all_to_all | solution.py:354
  125.8 3.8 %tri.3 = bf16[128,40,128]{2,1,0:T(8,128)(2,1)} custom-call(bf16[128,72,128]{2,1,0:T(8,128)(2,1)S(1)} %all-to-all-done.2.in_ref), custom_call_target="tpu_custom_call" | custom-call | tf_op jit(solution)/shard_map/tri/pallas_call | solution.py:315
  129.6 4.5 %all-to-all-start.3 = ((bf16[128,40,128]{2,1,0:T(8,128)(2,1)}), bf16[128,40,128]{2,1,0:T(8,128)(2,1)S(1)}, u32[]{:S(2)}, u32[]{:S(2)}) async-start(bf16[128,40,128]{2,1,0:T(8,128)(2,1)} %tri.3), calls=%async_computation.3 | async-start | bytes 2621440 | tf_op jit(solution)/shard_map/all_to_all | solution.py:354
  134.2 1.6 %fusion.10 = f32[48,96]{1,0:T(8,128)S(1)} fusion(bf16[48,96,128]{2,1,0:T(8,128)(2,1)S(1)} %copy-done.6, f32[48,96]{1,0:T(8,128)S(1)} %broadcast_multiply_fusion), kind=kLoop, calls=%fused_computation.16 | loop fusion | flops 2354688 | bytes 1216512 | tf_op jit(solution)/shard_map/reduce_sum | solution.py:23
  135.9 1.5 fusion.13
  137.4 2.2 %fusion.5 = f32[4608,128]{1,0:T(8,128)} fusion(bf16[4608,128]{1,0:T(8,128)(2,1)S(1)} %bitcast.23, bf16[2,128,640]{2,1,0:T(8,128)(2,1)S(1)} %copy-done), kind=kOutput, calls=%fused_computation.7 | convolution fusion | flops 152764416 | bytes 3571712 | tf_op jit(solution)/shard_map/dot_general | solution.py:348
  139.6 16.8 %all-to-all-done.3.prod = bf16[128,40,128]{2,1,0:T(8,128)(2,1)S(1)} async-done(((bf16[128,40,128]{2,1,0:T(8,128)(2,1)}), bf16[128,40,128]{2,1,0:T(8,128)(2,1)S(1)}, u32[]{:S(2)}, u32[]{:S(2)}) %all-to-all-start.3) | async-done | bytes 1310752 | tf_op jit(solution)/shard_map/all_to_all | solution.py:354
  156.4 3.7 %post.1 = bf16[48,96,128]{2,1,0:T(8,128)(2,1)} custom-call(bf16[128,40,128]{2,1,0:T(8,128)(2,1)S(1)} %all-to-all-done.3.prod, bf16[48,96,128]{2,1,0:T(8,128)(2,1)} %get-tuple-element.8.z_hbm, f32[48,96,128]{2,1,0:T(8,128)} %bitcast.21, f32[2,2,128]{2,1,0:T(2,128)S(1)} %copy-done.2, f32[2,2,128]{2,1,0:T(2,128)S(1)} %copy-done.3, ...), custom_call_target="tpu_custom_call" | custom-call | tf_op jit(solution)/shard_map/post/pallas_call | solution.py:315
  (8 shorter events, 0.0 us)
Async XLA Ops:
  5.1 44.8 %all-to-all-start = ((bf16[128,72,128]{2,1,0:T(8,128)(2,1)}), bf16[128,72,128]{2,1,0:T(8,128)(2,1)S(1)}, u32[]{:S(2)}, u32[]{:S(2)}) async-start(bf16[128,72,128]{2,1,0:T(8,128)(2,1)} %pre.1), calls=%async_computation | async-start | bytes 4718592 | tf_op jit(solution)/shard_map/all_to_all | solution.py:354
  53.7 7.4 %copy-start.2 = (f32[2,2,128]{2,1,0:T(2,128)S(1)}, f32[2,2,128]{2,1,0:T(2,128)}, u32[]{:S(2)}) copy-start(f32[2,2,128]{2,1,0:T(2,128)} %gains.3) | copy-start | bytes 6148
  53.7 7.3 %copy-start.3 = (f32[2,2,128]{2,1,0:T(2,128)S(1)}, f32[2,2,128]{2,1,0:T(2,128)}, u32[]{:S(2)}) copy-start(f32[2,2,128]{2,1,0:T(2,128)} %biases.3) | copy-start | bytes 6148
  53.7 7.4 %copy-start.5 = (bf16[48,96,128]{2,1,0:T(8,128)(2,1)S(1)}, bf16[48,96,128]{2,1,0:T(8,128)(2,1)}, u32[]{:S(2)}) copy-start(bf16[48,96,128]{2,1,0:T(8,128)(2,1)} %z_hbm.3) | copy-start | bytes 3538948
  53.7 26.7 %all-to-all-start.1 = ((bf16[128,40,128]{2,1,0:T(8,128)(2,1)}), bf16[128,40,128]{2,1,0:T(8,128)(2,1)S(1)}, u32[]{:S(2)}, u32[]{:S(2)}) async-start(bf16[128,40,128]{2,1,0:T(8,128)(2,1)} %tri.2), calls=%async_computation.1 | async-start | bytes 2621440 | tf_op jit(solution)/shard_map/all_to_all | solution.py:354
  58.3 4.3 %copy-start = (bf16[2,128,640]{2,1,0:T(8,128)(2,1)S(1)}, bf16[2,128,640]{2,1,0:T(8,128)(2,1)}, u32[]{:S(2)}) copy-start(bf16[2,128,640]{2,1,0:T(8,128)(2,1)} %w.1) | copy-start | bytes 983044
  62.6 17.9 %copy-start.1 = (bf16[2,128,128]{2,1,0:T(8,128)(2,1)S(1)}, bf16[2,128,128]{2,1,0:T(8,128)(2,1)}, u32[]{:S(2)}) copy-start(bf16[2,128,128]{2,1,0:T(8,128)(2,1)} %w_out.3) | copy-start | bytes 196612
  62.6 17.9 %copy-start.4 = (s32[8]{0:T(128)S(1)}, s32[8]{0:T(128)}, u32[]{:S(2)}) copy-start(s32[8]{0:T(128)} %chain.1) | copy-start | bytes 100
  88.0 37.8 %all-to-all-start.2 = ((bf16[128,72,128]{2,1,0:T(8,128)(2,1)}), bf16[128,72,128]{2,1,0:T(8,128)(2,1)S(1)}, u32[]{:S(2)}, u32[]{:S(2)}) async-start(bf16[128,72,128]{2,1,0:T(8,128)(2,1)} %get-tuple-element.7), calls=%async_computation.2 | async-start | bytes 4718592 | tf_op jit(solution)/shard_map/all_to_all | solution.py:354
  129.6 4.6 %copy-start.6 = (bf16[48,96,128]{2,1,0:T(8,128)(2,1)S(1)}, bf16[48,96,128]{2,1,0:T(8,128)(2,1)}, u32[]{:S(2)}) copy-start(bf16[48,96,128]{2,1,0:T(8,128)(2,1)} %get-tuple-element.8.z_hbm) | copy-start | bytes 3538948
  129.6 26.7 %all-to-all-start.3 = ((bf16[128,40,128]{2,1,0:T(8,128)(2,1)}), bf16[128,40,128]{2,1,0:T(8,128)(2,1)S(1)}, u32[]{:S(2)}, u32[]{:S(2)}) async-start(bf16[128,40,128]{2,1,0:T(8,128)(2,1)} %tri.3), calls=%async_computation.3 | async-start | bytes 2621440 | tf_op jit(solution)/shard_map/all_to_all | solution.py:354

commit v5 on v4

--- a/solution.py
+++ b/solution.py
@@ -13,6 +13,7 @@
 KHI, KLO = 3, 32
 NQ = 36
 SA, SP = 24, 40
+PARTS = 2
 BF, F32 = jnp.bfloat16, jnp.float32
 
 
@@ -173,8 +174,10 @@
     return project
 
 
-def factors_out(stage, out, sems, h):
-    return pltpu.make_async_copy(stage.at[h], out.at[:, pl.ds(pl.multiple_of(h * SA, SA), SA)], sems.at[h])
+def factors_out(stage, out, sems, h, part):
+    dests = pl.ds(part * (C // PARTS), C // PARTS)
+    return pltpu.make_async_copy(
+        stage.at[h, dests], out.at[dests, pl.ds(pl.multiple_of(h * SA, SA), SA)], sems.at[h, part])
 
 
 def send_factors(scr, stage, out, sems, h):
@@ -182,8 +185,9 @@
         stage[h, s] = scr[pl.ds(pl.multiple_of(s * SA, SA), SA), :].astype(BF)
         return carry
 
-    lax.fori_loop(0, C, cast, 0, unroll=32)
-    factors_out(stage, out, sems, h).start()
+    for part in range(PARTS):
+        lax.fori_loop(part * (C // PARTS), (part + 1) * (C // PARTS), cast, 0, unroll=32)
+        factors_out(stage, out, sems, h, part).start()
 
 
 def each_column(step):
@@ -191,7 +195,7 @@
         step(h)
         return carry
 
-    lax.fori_loop(0, KHI, one, 0)
+    lax.fori_loop(0, KHI, one, 0, unroll=True)
 
 
 def pre_kernel(chain_hbm, z_hbm, w_hbm, gain_hbm, bias_hbm, out_hbm,
@@ -213,10 +217,11 @@
 
     each_column(step)
     for h in range(KHI):
-        factors_out(stage, out_hbm, out_sems, h).wait()
-
-
-def post_parts(prod, z_hbm, gate_hbm, gains, biases, w_out, z, gate, wide, z_sems, gate_sems, u):
+        for part in range(PARTS):
+            factors_out(stage, out_hbm, out_sems, h, part).wait()
+
+
+def post_parts(prod, z_hbm, gate_hbm, gains, biases, w_out, z, gate, wide, normed, z_sems, gate_sems, u):
     for h in range(KHI):
         column_in(z_hbm, z, z_sems, h).start()
         column_in(gate_hbm, gate, gate_sems, h).start()
@@ -229,37 +234,40 @@
 
     lax.fori_loop(0, C, widen, 0, unroll=32)
 
-    def ready(h):
+    def normalise(h):
+        for part in range(3):
+            for e in range(4):
+                x = wide[pl.ds(product_row(part, h) + e, C, stride=SP), :]
+                mean = jnp.mean(x, axis=0, keepdims=True)
+                centred = x - mean
+                var = jnp.mean(centred * centred, axis=0, keepdims=True)
+                normed[h, 4 * part + e] = (centred * lax.rsqrt(var + 1e-05) * gain + bias).astype(BF)
+
+    each_column(normalise)
+
+    def update(z_out, h):
         column_in(z_hbm, z, z_sems, h).wait()
         column_in(gate_hbm, gate, gate_sems, h).wait()
-
-    def chunk(h, part, e):
-        row, gap = place(part)[:2]
-        x = wide[pl.ds(product_row(part, h) + e, C, stride=SP), :]
-        mean = jnp.mean(x, axis=0, keepdims=True)
-        centred = x - mean
-        var = jnp.mean(centred * centred, axis=0, keepdims=True)
-        normed = (centred * lax.rsqrt(var + 1e-05) * gain + bias).astype(BF)
-        mixed = lax.dot_general(
-            normed, w_out[u], (((0,), (0,)), ((), ())), preferred_element_type=F32)
-        old = load_chunk(z, row + e, gap, h).astype(F32)
-        return (old + load_chunk(gate, row + e, gap, h) * mixed).astype(BF)
-
-    return ready, chunk
-
-
-def mid_kernel(chain, prod, z_hbm, gate_hbm, w, gains, biases, w_out, z_out_hbm, out_hbm,
-               z, gate, wide, z_out, scr, stage, z_sems, gate_sems, zo_sems, out_sems):
-    ready, chunk = post_parts(
-        prod, z_hbm, gate_hbm, gains, biases, w_out, z, gate, wide, z_sems, gate_sems, 0)
-    project = projector(chain, w, gains, biases, scr, 1)
-
-    def update(h):
-        ready(h)
         for part in range(3):
             row, gap = place(part)[:2]
             for e in range(4):
-                store_chunk(z_out, row + e, gap, h, chunk(h, part, e))
+                mixed = lax.dot_general(
+                    normed[h, 4 * part + e], w_out[u], (((0,), (0,)), ((), ())), preferred_element_type=F32)
+                old = load_chunk(z, row + e, gap, h).astype(F32)
+                new = old + load_chunk(gate, row + e, gap, h) * mixed
+                store_chunk(z_out, row + e, gap, h, new.astype(BF))
+
+    return update
+
+
+def mid_kernel(chain, prod, z_hbm, gate_hbm, w, gains, biases, w_out, z_out_hbm, out_hbm,
+               z, gate, wide, normed, z_out, scr, stage, z_sems, gate_sems, zo_sems, out_sems):
+    update = post_parts(
+        prod, z_hbm, gate_hbm, gains, biases, w_out, z, gate, wide, normed, z_sems, gate_sems, 0)
+    project = projector(chain, w, gains, biases, scr, 1)
+
+    def renew(h):
+        update(z_out, h)
         column_in(z_out, z_out_hbm, zo_sems, h).start()
 
     def step(h):
@@ -268,24 +276,21 @@
             project([load_chunk(z_out, row + e, gap, h) for e in range(4)], h, part)
         send_factors(scr, stage, out_hbm, out_sems, h)
 
-    each_column(update)
+    each_column(renew)
     each_column(step)
     for h in range(KHI):
         column_in(z_out, z_out_hbm, zo_sems, h).wait()
-        factors_out(stage, out_hbm, out_sems, h).wait()
+        for part in range(PARTS):
+            factors_out(stage, out_hbm, out_sems, h, part).wait()
 
 
 def post_kernel(prod, z_hbm, gate_hbm, gains, biases, w_out, z_out_hbm,
-                z, gate, wide, z_out, z_sems, gate_sems, zo_sems):
-    ready, chunk = post_parts(
-        prod, z_hbm, gate_hbm, gains, biases, w_out, z, gate, wide, z_sems, gate_sems, 1)
+                z, gate, wide, normed, z_out, z_sems, gate_sems, zo_sems):
+    update = post_parts(
+        prod, z_hbm, gate_hbm, gains, biases, w_out, z, gate, wide, normed, z_sems, gate_sems, 1)
 
     def step(h):
-        ready(h)
-        for part in range(3):
-            row, gap = place(part)[:2]
-            for e in range(4):
-                store_chunk(z_out, row + e, gap, h, chunk(h, part, e))
+        update(z_out, h)
         column_in(z_out, z_out_hbm, zo_sems, h).start()
 
     each_column(step)
@@ -306,7 +311,7 @@
         out_shape=shapes if len(shapes) > 1 else shapes[0],
         in_specs=in_specs,
         out_specs=[HBM] * len(shapes) if len(shapes) > 1 else HBM,
-        scratch_shapes=list(scratch) + [pltpu.SemaphoreType.DMA((n,)) for n in sems],
+        scratch_shapes=list(scratch) + [pltpu.SemaphoreType.DMA(n if isinstance(n, tuple) else (n,)) for n in sems],
         compiler_params=pltpu.CompilerParams(vmem_limit_bytes=limit << 20),
         name=name,
     )
@@ -327,16 +332,16 @@
     pre = call(
         pre_kernel, "pre", [FACTORS],
         [pltpu.SMEM((8,), jnp.int32), V(*STATE), V((2, C, 5 * C), BF), V((2, 2, C), F32), V((2, 2, C), F32)] + send,
-        [4, KHI, KHI], 20, [HBM] * 5)
+        [4, KHI, (KHI, PARTS)], 20, [HBM] * 5)
     tri = [
         call(
             functools.partial(tri_kernel, incoming=u == 1), "tri", [PRODUCTS],
             [V((N, N), BF), V((N, N), BF), V((N, N), F32), V(*PRODUCTS)], [ROWS // 2], 20, [VMEM])
         for u in range(2)
     ]
-    take = [V(*STATE), V(STATE[0], F32), V((C * SP, C), F32), V(*STATE)]
+    take = [V(*STATE), V(STATE[0], F32), V((C * SP, C), F32), V((KHI, 12, C, C), BF), V(*STATE)]
     mid = call(
-        mid_kernel, "mid", [STATE, FACTORS], take + send, [KHI, KHI, KHI, KHI], 26,
+        mid_kernel, "mid", [STATE, FACTORS], take + send, [KHI, KHI, KHI, (KHI, PARTS)], 26,
         [SMEM, VMEM] + [HBM] * 2 + [VMEM] * 4)
     post = call(
         post_kernel, "post", [STATE], take, [KHI, KHI, KHI], 16, [VMEM] + [HBM] * 2 + [VMEM] * 3)

time: 161 us -> 159 us (0.988)
  no operation moved by 1% of the time
where the time goes in v5:
time: 159 us
  waiting for transfers between devices  95.6 us (60%)
  starting transfers between devices  25 us (16%)
  Pallas kernels  22.4 us (14%)
  other arithmetic  10.9 us (7%)
  matrix products  4.38 us (3%)
    all_to_all x4, waiting for transfers between devices, exchange(): return lax.all_to_all(blocks, ('row', 'col'), 0, 0, tiled=True)  95.6 us
    all_to_all x4, starting transfers between devices, exchange(): return lax.all_to_all(blocks, ('row', 'col'), 0, 0, tiled=True)  25 us
    pallas_call x5, Pallas kernels, placed(): run(*(pltpu.with_memory_space_constraint(a, s.memory_space) if s is HBM o...  22.4 us
    reduce_sum x2, other arithmetic, norm_rows(): var = jnp.mean(centred * centred, axis=1, keepdims=True)  4.39 us
    dot_general x2, matrix products, output_gate(): jnp.dot(normed, w_in[u, :, 4 * C:], preferred_element_type=F32)  4.38 us
    reduce_sum x2, other arithmetic, norm_rows(): mean = jnp.mean(wide, axis=1, keepdims=True)  3.52 us
  transfers between devices with their start and end apart: 4, of which 4 were waited for; matrix products, arithmetic and copies ran while one was open for 10% of the time, Pallas kernels for 0%

profile of v5, /device:TPU:1, one launch (start us, length us, event | category | flops | bytes accessed | tf_op | source)
XLA Modules:
  0.0 158.7 jit_solution(5040667292683743393)
XLA Ops:
  0.0 5.1 %pre.1 = bf16[128,72,128]{2,1,0:T(8,128)(2,1)} custom-call(s32[8]{0:T(128)} %chain.1, bf16[48,96,128]{2,1,0:T(8,128)(2,1)} %z_hbm.3, bf16[2,128,640]{2,1,0:T(8,128)(2,1)} %w.1, f32[2,2,128]{2,1,0:T(2,128)} %gains.3, f32[2,2,128]{2,1,0:T(2,128)} %biases.3), custom_call_target="tpu_custom_call" | custom-call | tf_op jit(solution)/shard_map/pre/pallas_call | solution.py:320
  5.1 11.5 %all-to-all-start = ((bf16[128,72,128]{2,1,0:T(8,128)(2,1)}), bf16[128,72,128]{2,1,0:T(8,128)(2,1)S(1)}, u32[]{:S(2)}, u32[]{:S(2)}) async-start(bf16[128,72,128]{2,1,0:T(8,128)(2,1)} %pre.1), calls=%async_computation | async-start | bytes 4718592 | tf_op jit(solution)/shard_map/all_to_all | solution.py:359
  16.6 1.8 %convert_reduce_fusion.1 = f32[48,96]{1,0:T(8,128)S(1)} fusion(bf16[48,96,128]{2,1,0:T(8,128)(2,1)} %z_hbm.3), kind=kLoop, calls=%fused_computation.11 | loop fusion | flops 1175040 | bytes 1198080 | tf_op jit(solution)/shard_map/reduce_sum | solution.py:22
  18.3 31.5 %all-to-all-done.in_ref = bf16[128,72,128]{2,1,0:T(8,128)(2,1)S(1)} async-done(((bf16[128,72,128]{2,1,0:T(8,128)(2,1)}), bf16[128,72,128]{2,1,0:T(8,128)(2,1)S(1)}, u32[]{:S(2)}, u32[]{:S(2)}) %all-to-all-start) | async-done | bytes 2359328 | tf_op jit(solution)/shard_map/all_to_all | solution.py:359
  49.8 3.8 %tri.2 = bf16[128,40,128]{2,1,0:T(8,128)(2,1)} custom-call(bf16[128,72,128]{2,1,0:T(8,128)(2,1)S(1)} %all-to-all-done.in_ref), custom_call_target="tpu_custom_call" | custom-call | tf_op jit(solution)/shard_map/tri/pallas_call | solution.py:320
  53.7 0.0 copy-start.2
  53.7 0.0 copy-start.3
  53.7 0.0 copy-start.5
  53.7 4.5 %all-to-all-start.1 = ((bf16[128,40,128]{2,1,0:T(8,128)(2,1)}), bf16[128,40,128]{2,1,0:T(8,128)(2,1)S(1)}, u32[]{:S(2)}, u32[]{:S(2)}) async-start(bf16[128,40,128]{2,1,0:T(8,128)(2,1)} %tri.2), calls=%async_computation.1 | async-start | bytes 2621440 | tf_op jit(solution)/shard_map/all_to_all | solution.py:359
  58.3 0.0 copy-start
  58.3 2.7 %fusion.14 = f32[48,96]{1,0:T(8,128)S(1)} fusion(bf16[48,96,128]{2,1,0:T(8,128)(2,1)} %z_hbm.3, f32[48,96]{1,0:T(8,128)S(1)} %broadcast_multiply_fusion.1), kind=kLoop, calls=%fused_computation.20 | loop fusion | flops 2354688 | bytes 1216512 | tf_op jit(solution)/shard_map/reduce_sum | solution.py:24
  61.0 0.0 copy-done.2
  61.0 0.0 copy-done.3
  61.1 0.0 copy-done.5
  61.1 1.5 fusion.17
  62.6 0.0 copy-start.1
  62.6 0.0 copy-start.4
  62.6 2.2 %fusion.4 = f32[4608,128]{1,0:T(8,128)} fusion(bf16[4608,128]{1,0:T(8,128)(2,1)S(1)} %bitcast.22, bf16[2,128,640]{2,1,0:T(8,128)(2,1)S(1)} %copy-done), kind=kOutput, calls=%fused_computation.6 | convolution fusion | flops 152764416 | bytes 3571712 | tf_op jit(solution)/shard_map/dot_general | solution.py:353
  64.8 15.6 %all-to-all-done.1.prod = bf16[128,40,128]{2,1,0:T(8,128)(2,1)S(1)} async-done(((bf16[128,40,128]{2,1,0:T(8,128)(2,1)}), bf16[128,40,128]{2,1,0:T(8,128)(2,1)S(1)}, u32[]{:S(2)}, u32[]{:S(2)}) %all-to-all-start.1) | async-done | bytes 1310752 | tf_op jit(solution)/shard_map/all_to_all | solution.py:359
  80.4 0.0 copy-done.4
  80.4 6.6 %mid.1 = (bf16[48,96,128]{2,1,0:T(8,128)(2,1)}, bf16[128,72,128]{2,1,0:T(8,128)(2,1)}) custom-call(s32[8]{0:T(128)S(1)} %copy-done.4, bf16[128,40,128]{2,1,0:T(8,128)(2,1)S(1)} %all-to-all-done.1.prod, bf16[48,96,128]{2,1,0:T(8,128)(2,1)} %z_hbm.3, f32[48,96,128]{2,1,0:T(8,128)} %bitcast.20, bf16[2,128,640]{2,1,0:T(8,128)(2,1)S(1)} %copy-done, ...), custom_call_target="tpu_custom_call" | custom-call | tf_op jit(solution)/shard_map/mid/pallas_call | solution.py:320
  87.1 4.4 %all-to-all-start.2 = ((bf16[128,72,128]{2,1,0:T(8,128)(2,1)}), bf16[128,72,128]{2,1,0:T(8,128)(2,1)S(1)}, u32[]{:S(2)}, u32[]{:S(2)}) async-start(bf16[128,72,128]{2,1,0:T(8,128)(2,1)} %get-tuple-element.7), calls=%async_computation.2 | async-start | bytes 4718592 | tf_op jit(solution)/shard_map/all_to_all | solution.py:359
  91.5 1.8 %convert_reduce_fusion = f32[48,96]{1,0:T(8,128)S(1)} fusion(bf16[48,96,128]{2,1,0:T(8,128)(2,1)} %get-tuple-element.8.z_hbm), kind=kLoop, calls=%fused_computation.9 | loop fusion | flops 1175040 | bytes 1198080 | tf_op jit(solution)/shard_map/reduce_sum | solution.py:22
  93.2 31.6 %all-to-all-done.2.in_ref = bf16[128,72,128]{2,1,0:T(8,128)(2,1)S(1)} async-done(((bf16[128,72,128]{2,1,0:T(8,128)(2,1)}), bf16[128,72,128]{2,1,0:T(8,128)(2,1)S(1)}, u32[]{:S(2)}, u32[]{:S(2)}) %all-to-all-start.2) | async-done | bytes 2359328 | tf_op jit(solution)/shard_map/all_to_all | solution.py:359
  124.9 3.8 %tri.3 = bf16[128,40,128]{2,1,0:T(8,128)(2,1)} custom-call(bf16[128,72,128]{2,1,0:T(8,128)(2,1)S(1)} %all-to-all-done.2.in_ref), custom_call_target="tpu_custom_call" | custom-call | tf_op jit(solution)/shard_map/tri/pallas_call | solution.py:320
  128.7 0.0 copy-start.6
  128.7 4.5 %all-to-all-start.3 = ((bf16[128,40,128]{2,1,0:T(8,128)(2,1)}), bf16[128,40,128]{2,1,0:T(8,128)(2,1)S(1)}, u32[]{:S(2)}, u32[]{:S(2)}) async-start(bf16[128,40,128]{2,1,0:T(8,128)(2,1)} %tri.3), calls=%async_computation.3 | async-start | bytes 2621440 | tf_op jit(solution)/shard_map/all_to_all | solution.py:359
  133.3 1.6 %fusion.10 = f32[48,96]{1,0:T(8,128)S(1)} fusion(bf16[48,96,128]{2,1,0:T(8,128)(2,1)S(1)} %copy-done.6, f32[48,96]{1,0:T(8,128)S(1)} %broadcast_multiply_fusion), kind=kLoop, calls=%fused_computation.16 | loop fusion | flops 2354688 | bytes 1216512 | tf_op jit(solution)/shard_map/reduce_sum | solution.py:24
  135.0 1.5 fusion.13
  136.4 2.2 %fusion.5 = f32[4608,128]{1,0:T(8,128)} fusion(bf16[4608,128]{1,0:T(8,128)(2,1)S(1)} %bitcast.23, bf16[2,128,640]{2,1,0:T(8,128)(2,1)S(1)} %copy-done), kind=kOutput, calls=%fused_computation.7 | convolution fusion | flops 152764416 | bytes 3571712 | tf_op jit(solution)/shard_map/dot_general | solution.py:353
  138.6 16.8 %all-to-all-done.3.prod = bf16[128,40,128]{2,1,0:T(8,128)(2,1)S(1)} async-done(((bf16[128,40,128]{2,1,0:T(8,128)(2,1)}), bf16[128,40,128]{2,1,0:T(8,128)(2,1)S(1)}, u32[]{:S(2)}, u32[]{:S(2)}) %all-to-all-start.3) | async-done | bytes 1310752 | tf_op jit(solution)/shard_map/all_to_all | solution.py:359
  155.4 3.1 %post.1 = bf16[48,96,128]{2,1,0:T(8,128)(2,1)} custom-call(bf16[128,40,128]{2,1,0:T(8,128)(2,1)S(1)} %all-to-all-done.3.prod, bf16[48,96,128]{2,1,0:T(8,128)(2,1)} %get-tuple-element.8.z_hbm, f32[48,96,128]{2,1,0:T(8,128)} %bitcast.21, f32[2,2,128]{2,1,0:T(2,128)S(1)} %copy-done.2, f32[2,2,128]{2,1,0:T(2,128)S(1)} %copy-done.3, ...), custom_call_target="tpu_custom_call" | custom-call | tf_op jit(solution)/shard_map/post/pallas_call | solution.py:320
  (8 shorter events, 0.0 us)
Async XLA Ops:
  5.1 44.8 %all-to-all-start = ((bf16[128,72,128]{2,1,0:T(8,128)(2,1)}), bf16[128,72,128]{2,1,0:T(8,128)(2,1)S(1)}, u32[]{:S(2)}, u32[]{:S(2)}) async-start(bf16[128,72,128]{2,1,0:T(8,128)(2,1)} %pre.1), calls=%async_computation | async-start | bytes 4718592 | tf_op jit(solution)/shard_map/all_to_all | solution.py:359
  53.7 7.4 %copy-start.2 = (f32[2,2,128]{2,1,0:T(2,128)S(1)}, f32[2,2,128]{2,1,0:T(2,128)}, u32[]{:S(2)}) copy-start(f32[2,2,128]{2,1,0:T(2,128)} %gains.3) | copy-start | bytes 6148
  53.7 7.4 %copy-start.3 = (f32[2,2,128]{2,1,0:T(2,128)S(1)}, f32[2,2,128]{2,1,0:T(2,128)}, u32[]{:S(2)}) copy-start(f32[2,2,128]{2,1,0:T(2,128)} %biases.3) | copy-start | bytes 6148
  53.7 7.4 %copy-start.5 = (bf16[48,96,128]{2,1,0:T(8,128)(2,1)S(1)}, bf16[48,96,128]{2,1,0:T(8,128)(2,1)}, u32[]{:S(2)}) copy-start(bf16[48,96,128]{2,1,0:T(8,128)(2,1)} %z_hbm.3) | copy-start | bytes 3538948
  53.7 26.7 %all-to-all-start.1 = ((bf16[128,40,128]{2,1,0:T(8,128)(2,1)}), bf16[128,40,128]{2,1,0:T(8,128)(2,1)S(1)}, u32[]{:S(2)}, u32[]{:S(2)}) async-start(bf16[128,40,128]{2,1,0:T(8,128)(2,1)} %tri.2), calls=%async_computation.1 | async-start | bytes 2621440 | tf_op jit(solution)/shard_map/all_to_all | solution.py:359
  58.3 4.3 %copy-start = (bf16[2,128,640]{2,1,0:T(8,128)(2,1)S(1)}, bf16[2,128,640]{2,1,0:T(8,128)(2,1)}, u32[]{:S(2)}) copy-start(bf16[2,128,640]{2,1,0:T(8,128)(2,1)} %w.1) | copy-start | bytes 983044
  62.6 17.9 %copy-start.1 = (bf16[2,128,128]{2,1,0:T(8,128)(2,1)S(1)}, bf16[2,128,128]{2,1,0:T(8,128)(2,1)}, u32[]{:S(2)}) copy-start(bf16[2,128,128]{2,1,0:T(8,128)(2,1)} %w_out.3) | copy-start | bytes 196612
  62.6 17.8 %copy-start.4 = (s32[8]{0:T(128)S(1)}, s32[8]{0:T(128)}, u32[]{:S(2)}) copy-start(s32[8]{0:T(128)} %chain.1) | copy-start | bytes 100
  87.1 37.8 %all-to-all-start.2 = ((bf16[128,72,128]{2,1,0:T(8,128)(2,1)}), bf16[128,72,128]{2,1,0:T(8,128)(2,1)S(1)}, u32[]{:S(2)}, u32[]{:S(2)}) async-start(bf16[128,72,128]{2,1,0:T(8,128)(2,1)} %get-tuple-element.7), calls=%async_computation.2 | async-start | bytes 4718592 | tf_op jit(solution)/shard_map/all_to_all | solution.py:359
  128.7 4.6 %copy-start.6 = (bf16[48,96,128]{2,1,0:T(8,128)(2,1)S(1)}, bf16[48,96,128]{2,1,0:T(8,128)(2,1)}, u32[]{:S(2)}) copy-start(bf16[48,96,128]{2,1,0:T(8,128)(2,1)} %get-tuple-element.8.z_hbm) | copy-start | bytes 3538948
  128.7 26.7 %all-to-all-start.3 = ((bf16[128,40,128]{2,1,0:T(8,128)(2,1)}), bf16[128,40,128]{2,1,0:T(8,128)(2,1)S(1)}, u32[]{:S(2)}, u32[]{:S(2)}) async-start(bf16[128,40,128]{2,1,0:T(8,128)(2,1)} %tri.3), calls=%async_computation.3 | async-start | bytes 2621440 | tf_op jit(solution)/shard_map/all_to_all | solution.py:359

commit v6 on v5

--- a/solution.py
+++ b/solution.py
@@ -97,8 +97,10 @@
                 [jnp.where(top, pltpu.roll(j[0], 4, 0), j[1]), pltpu.roll(j[2], 4, 0)],
             )
             for e in range(2):
-                block = jnp.concatenate(main[e][KHI * c:KHI * c + KHI] + last[e], axis=0)
-                stage[rs[e] * COLS + c] = block.astype(BF)
+                for n, piece in enumerate(main[e][KHI * c:KHI * c + KHI] + last[e]):
+                    for half in range(2 if n < 4 else 1):
+                        at = (2 * n + half) * C
+                        stage[rs[e] * COLS + c, :, at:at + C] = piece[4 * half:4 * half + 4].astype(BF)
         copy_out(t).start()
         return carry
 
@@ -229,7 +231,8 @@
     bias = jnp.broadcast_to(biases[u, 1:2, :], (C, C)).T
 
     def widen(s, carry):
-        wide[pl.ds(pl.multiple_of(s * SP, 8), SP), :] = prod[s].astype(F32)
+        fours = [prod[s, :, n * C:(n + 1) * C].astype(F32) for n in range(NQ // 4)]
+        wide[pl.ds(pl.multiple_of(s * SP, 8), NQ), :] = jnp.concatenate(fours, axis=0)
         return carry
 
     lax.fori_loop(0, C, widen, 0, unroll=32)
@@ -301,7 +304,7 @@
 HBM = pl.BlockSpec(memory_space=pltpu.HBM)
 VMEM = pl.BlockSpec(memory_space=pltpu.VMEM)
 SMEM = pl.BlockSpec(memory_space=pltpu.SMEM)
-FACTORS, PRODUCTS, STATE = ((C, 2 * NQ, C), BF), ((C, SP, C), BF), ((TR, TC, C), BF)
+FACTORS, PRODUCTS, STATE = ((C, 2 * NQ, C), BF), ((C, 4, NQ // 4 * C), BF), ((TR, TC, C), BF)
 
 
 def call(kernel, name, outs, scratch, sems, limit, in_specs):

time: 159 us -> 157 us (0.987)
  waiting for transfers between devices: 95.6 us -> 92.8 us
    all_to_all x4, waiting for transfers between devices: 95.6 us -> 92.8 us  [exchange(): return lax.all_to_all(blocks, ('row', 'col'), 0, 0, tiled=True)]
where the time goes in v6:
time: 157 us; the launch traced here: 156 us
  waiting for transfers between devices  92.8 us (59%)
  starting transfers between devices  25 us (16%)
  Pallas kernels  22.7 us (14%)
  other arithmetic  10.9 us (7%)
  matrix products  4.39 us (3%)
    all_to_all x4, waiting for transfers between devices, exchange(): return lax.all_to_all(blocks, ('row', 'col'), 0, 0, tiled=True)  92.8 us
    all_to_all x4, starting transfers between devices, exchange(): return lax.all_to_all(blocks, ('row', 'col'), 0, 0, tiled=True)  25 us
    pallas_call x5, Pallas kernels, placed(): run(*(pltpu.with_memory_space_constraint(a, s.memory_space) if s is HBM o...  22.7 us
    reduce_sum x2, other arithmetic, norm_rows(): var = jnp.mean(centred * centred, axis=1, keepdims=True)  4.39 us
    dot_general x2, matrix products, output_gate(): jnp.dot(normed, w_in[u, :, 4 * C:], preferred_element_type=F32)  4.39 us
    reduce_sum x2, other arithmetic, norm_rows(): mean = jnp.mean(wide, axis=1, keepdims=True)  3.52 us
  transfers between devices with their start and end apart: 4, of which 4 were waited for; matrix products, arithmetic and copies ran while one was open for 10% of the time, Pallas kernels for 0%

profile of v6, /device:TPU:1, one launch (start us, length us, event | category | flops | bytes accessed | tf_op | source)
XLA Modules:
  0.0 156.2 jit_solution(7818162072462711384)
XLA Ops:
  0.0 5.1 %pre.1 = bf16[128,72,128]{2,1,0:T(8,128)(2,1)} custom-call(s32[8]{0:T(128)} %chain.1, bf16[48,96,128]{2,1,0:T(8,128)(2,1)} %z_hbm.3, bf16[2,128,640]{2,1,0:T(8,128)(2,1)} %w.1, f32[2,2,128]{2,1,0:T(2,128)} %gains.3, f32[2,2,128]{2,1,0:T(2,128)} %biases.3), custom_call_target="tpu_custom_call" | custom-call | tf_op jit(solution)/shard_map/pre/pallas_call | solution.py:323
  5.1 11.5 %all-to-all-start = ((bf16[128,72,128]{2,1,0:T(8,128)(2,1)}), bf16[128,72,128]{2,1,0:T(8,128)(2,1)S(1)}, u32[]{:S(2)}, u32[]{:S(2)}) async-start(bf16[128,72,128]{2,1,0:T(8,128)(2,1)} %pre.1), calls=%async_computation | async-start | bytes 4718592 | tf_op jit(solution)/shard_map/all_to_all | solution.py:362
  16.6 1.8 %convert_reduce_fusion.1 = f32[48,96]{1,0:T(8,128)S(1)} fusion(bf16[48,96,128]{2,1,0:T(8,128)(2,1)} %z_hbm.3), kind=kLoop, calls=%fused_computation.11 | loop fusion | flops 1175040 | bytes 1198080 | tf_op jit(solution)/shard_map/reduce_sum | solution.py:22
  18.3 31.5 %all-to-all-done.in_ref = bf16[128,72,128]{2,1,0:T(8,128)(2,1)S(1)} async-done(((bf16[128,72,128]{2,1,0:T(8,128)(2,1)}), bf16[128,72,128]{2,1,0:T(8,128)(2,1)S(1)}, u32[]{:S(2)}, u32[]{:S(2)}) %all-to-all-start) | async-done | bytes 2359328 | tf_op jit(solution)/shard_map/all_to_all | solution.py:362
  49.8 4.0 %tri.2 = bf16[128,4,1152]{2,1,0:T(4,128)(2,1)} custom-call(bf16[128,72,128]{2,1,0:T(8,128)(2,1)S(1)} %all-to-all-done.in_ref), custom_call_target="tpu_custom_call" | custom-call | tf_op jit(solution)/shard_map/tri/pallas_call | solution.py:323
  53.8 0.0 copy-start.2
  53.8 0.0 copy-start.3
  53.8 0.0 copy-start.5
  53.9 4.5 %all-to-all-start.1 = ((bf16[128,4,1152]{2,1,0:T(4,128)(2,1)}), bf16[128,4,1152]{2,1,0:T(4,128)(2,1)S(1)}, u32[]{:S(2)}, u32[]{:S(2)}) async-start(bf16[128,4,1152]{2,1,0:T(4,128)(2,1)} %tri.2), calls=%async_computation.1 | async-start | bytes 2359296 | tf_op jit(solution)/shard_map/all_to_all | solution.py:362
  58.4 0.0 copy-start
  58.4 2.7 %fusion.14 = f32[48,96]{1,0:T(8,128)S(1)} fusion(bf16[48,96,128]{2,1,0:T(8,128)(2,1)} %z_hbm.3, f32[48,96]{1,0:T(8,128)S(1)} %broadcast_multiply_fusion.1), kind=kLoop, calls=%fused_computation.20 | loop fusion | flops 2354688 | bytes 1216512 | tf_op jit(solution)/shard_map/reduce_sum | solution.py:24
  61.2 0.0 copy-done.2
  61.2 0.0 copy-done.3
  61.2 0.0 copy-done.5
  61.2 1.5 fusion.17
  62.7 0.0 copy-done
  62.7 0.0 copy-start.1
  62.7 0.0 copy-start.4
  62.7 2.2 %fusion.4 = f32[4608,128]{1,0:T(8,128)} fusion(bf16[4608,128]{1,0:T(8,128)(2,1)S(1)} %bitcast.22, bf16[2,128,640]{2,1,0:T(8,128)(2,1)S(1)} %copy-done), kind=kOutput, calls=%fused_computation.6 | convolution fusion | flops 152764416 | bytes 3571712 | tf_op jit(solution)/shard_map/dot_general | solution.py:356
  64.9 14.2 %all-to-all-done.1.prod = bf16[128,4,1152]{2,1,0:T(4,128)(2,1)S(1)} async-done(((bf16[128,4,1152]{2,1,0:T(4,128)(2,1)}), bf16[128,4,1152]{2,1,0:T(4,128)(2,1)S(1)}, u32[]{:S(2)}, u32[]{:S(2)}) %all-to-all-start.1) | async-done | bytes 1179680 | tf_op jit(solution)/shard_map/all_to_all | solution.py:362
  79.2 0.0 copy-done.1
  79.2 6.6 %mid.1 = (bf16[48,96,128]{2,1,0:T(8,128)(2,1)}, bf16[128,72,128]{2,1,0:T(8,128)(2,1)}) custom-call(s32[8]{0:T(128)S(1)} %copy-done.4, bf16[128,4,1152]{2,1,0:T(4,128)(2,1)S(1)} %all-to-all-done.1.prod, bf16[48,96,128]{2,1,0:T(8,128)(2,1)} %z_hbm.3, f32[48,96,128]{2,1,0:T(8,128)} %bitcast.20, bf16[2,128,640]{2,1,0:T(8,128)(2,1)S(1)} %copy-done, ...), custom_call_target="tpu_custom_call" | custom-call | tf_op jit(solution)/shard_map/mid/pallas_call | solution.py:323
  85.8 4.4 %all-to-all-start.2 = ((bf16[128,72,128]{2,1,0:T(8,128)(2,1)}), bf16[128,72,128]{2,1,0:T(8,128)(2,1)S(1)}, u32[]{:S(2)}, u32[]{:S(2)}) async-start(bf16[128,72,128]{2,1,0:T(8,128)(2,1)} %get-tuple-element.7), calls=%async_computation.2 | async-start | bytes 4718592 | tf_op jit(solution)/shard_map/all_to_all | solution.py:362
  90.2 1.8 %convert_reduce_fusion = f32[48,96]{1,0:T(8,128)S(1)} fusion(bf16[48,96,128]{2,1,0:T(8,128)(2,1)} %get-tuple-element.8.z_hbm), kind=kLoop, calls=%fused_computation.9 | loop fusion | flops 1175040 | bytes 1198080 | tf_op jit(solution)/shard_map/reduce_sum | solution.py:22
  92.0 31.6 %all-to-all-done.2.in_ref = bf16[128,72,128]{2,1,0:T(8,128)(2,1)S(1)} async-done(((bf16[128,72,128]{2,1,0:T(8,128)(2,1)}), bf16[128,72,128]{2,1,0:T(8,128)(2,1)S(1)}, u32[]{:S(2)}, u32[]{:S(2)}) %all-to-all-start.2) | async-done | bytes 2359328 | tf_op jit(solution)/shard_map/all_to_all | solution.py:362
  123.6 4.0 %tri.3 = bf16[128,4,1152]{2,1,0:T(4,128)(2,1)} custom-call(bf16[128,72,128]{2,1,0:T(8,128)(2,1)S(1)} %all-to-all-done.2.in_ref), custom_call_target="tpu_custom_call" | custom-call | tf_op jit(solution)/shard_map/tri/pallas_call | solution.py:323
  127.6 4.6 %all-to-all-start.3 = ((bf16[128,4,1152]{2,1,0:T(4,128)(2,1)}), bf16[128,4,1152]{2,1,0:T(4,128)(2,1)S(1)}, u32[]{:S(2)}, u32[]{:S(2)}) async-start(bf16[128,4,1152]{2,1,0:T(4,128)(2,1)} %tri.3), calls=%async_computation.3 | async-start | bytes 2359296 | tf_op jit(solution)/shard_map/all_to_all | solution.py:362
  132.2 1.6 %fusion.10 = f32[48,96]{1,0:T(8,128)S(1)} fusion(bf16[48,96,128]{2,1,0:T(8,128)(2,1)S(1)} %copy-done.6, f32[48,96]{1,0:T(8,128)S(1)} %broadcast_multiply_fusion), kind=kLoop, calls=%fused_computation.16 | loop fusion | flops 2354688 | bytes 1216512 | tf_op jit(solution)/shard_map/reduce_sum | solution.py:24
  133.9 1.5 fusion.13
  135.4 2.2 %fusion.5 = f32[4608,128]{1,0:T(8,128)} fusion(bf16[4608,128]{1,0:T(8,128)(2,1)S(1)} %bitcast.23, bf16[2,128,640]{2,1,0:T(8,128)(2,1)S(1)} %copy-done), kind=kOutput, calls=%fused_computation.7 | convolution fusion | flops 152764416 | bytes 3571712 | tf_op jit(solution)/shard_map/dot_general | solution.py:356
  137.6 15.4 %all-to-all-done.3.prod = bf16[128,4,1152]{2,1,0:T(4,128)(2,1)S(1)} async-done(((bf16[128,4,1152]{2,1,0:T(4,128)(2,1)}), bf16[128,4,1152]{2,1,0:T(4,128)(2,1)S(1)}, u32[]{:S(2)}, u32[]{:S(2)}) %all-to-all-start.3) | async-done | bytes 1179680 | tf_op jit(solution)/shard_map/all_to_all | solution.py:362
  153.0 3.1 %post.1 = bf16[48,96,128]{2,1,0:T(8,128)(2,1)} custom-call(bf16[128,4,1152]{2,1,0:T(4,128)(2,1)S(1)} %all-to-all-done.3.prod, bf16[48,96,128]{2,1,0:T(8,128)(2,1)} %get-tuple-element.8.z_hbm, f32[48,96,128]{2,1,0:T(8,128)} %bitcast.21, f32[2,2,128]{2,1,0:T(2,128)S(1)} %copy-done.2, f32[2,2,128]{2,1,0:T(2,128)S(1)} %copy-done.3, ...), custom_call_target="tpu_custom_call" | custom-call | tf_op jit(solution)/shard_map/post/pallas_call | solution.py:323
  (8 shorter events, 0.0 us)
Async XLA Ops:
  5.1 44.8 %all-to-all-start = ((bf16[128,72,128]{2,1,0:T(8,128)(2,1)}), bf16[128,72,128]{2,1,0:T(8,128)(2,1)S(1)}, u32[]{:S(2)}, u32[]{:S(2)}) async-start(bf16[128,72,128]{2,1,0:T(8,128)(2,1)} %pre.1), calls=%async_computation | async-start | bytes 4718592 | tf_op jit(solution)/shard_map/all_to_all | solution.py:362
  53.8 7.4 %copy-start.2 = (f32[2,2,128]{2,1,0:T(2,128)S(1)}, f32[2,2,128]{2,1,0:T(2,128)}, u32[]{:S(2)}) copy-start(f32[2,2,128]{2,1,0:T(2,128)} %gains.3) | copy-start | bytes 6148
  53.8 7.4 %copy-start.3 = (f32[2,2,128]{2,1,0:T(2,128)S(1)}, f32[2,2,128]{2,1,0:T(2,128)}, u32[]{:S(2)}) copy-start(f32[2,2,128]{2,1,0:T(2,128)} %biases.3) | copy-start | bytes 6148
  53.8 7.4 %copy-start.5 = (bf16[48,96,128]{2,1,0:T(8,128)(2,1)S(1)}, bf16[48,96,128]{2,1,0:T(8,128)(2,1)}, u32[]{:S(2)}) copy-start(bf16[48,96,128]{2,1,0:T(8,128)(2,1)} %z_hbm.3) | copy-start | bytes 3538948
  53.9 25.3 %all-to-all-start.1 = ((bf16[128,4,1152]{2,1,0:T(4,128)(2,1)}), bf16[128,4,1152]{2,1,0:T(4,128)(2,1)S(1)}, u32[]{:S(2)}, u32[]{:S(2)}) async-start(bf16[128,4,1152]{2,1,0:T(4,128)(2,1)} %tri.2), calls=%async_computation.1 | async-start | bytes 2359296 | tf_op jit(solution)/shard_map/all_to_all | solution.py:362
  58.4 4.3 %copy-start = (bf16[2,128,640]{2,1,0:T(8,128)(2,1)S(1)}, bf16[2,128,640]{2,1,0:T(8,128)(2,1)}, u32[]{:S(2)}) copy-start(bf16[2,128,640]{2,1,0:T(8,128)(2,1)} %w.1) | copy-start | bytes 983044
  62.7 16.4 %copy-start.1 = (bf16[2,128,128]{2,1,0:T(8,128)(2,1)S(1)}, bf16[2,128,128]{2,1,0:T(8,128)(2,1)}, u32[]{:S(2)}) copy-start(bf16[2,128,128]{2,1,0:T(8,128)(2,1)} %w_out.3) | copy-start | bytes 196612
  62.7 16.4 %copy-start.4 = (s32[8]{0:T(128)S(1)}, s32[8]{0:T(128)}, u32[]{:S(2)}) copy-start(s32[8]{0:T(128)} %chain.1) | copy-start | bytes 100
  85.8 37.9 %all-to-all-start.2 = ((bf16[128,72,128]{2,1,0:T(8,128)(2,1)}), bf16[128,72,128]{2,1,0:T(8,128)(2,1)S(1)}, u32[]{:S(2)}, u32[]{:S(2)}) async-start(bf16[128,72,128]{2,1,0:T(8,128)(2,1)} %get-tuple-element.7), calls=%async_computation.2 | async-start | bytes 4718592 | tf_op jit(solution)/shard_map/all_to_all | solution.py:362
  127.6 4.6 %copy-start.6 = (bf16[48,96,128]{2,1,0:T(8,128)(2,1)S(1)}, bf16[48,96,128]{2,1,0:T(8,128)(2,1)}, u32[]{:S(2)}) copy-start(bf16[48,96,128]{2,1,0:T(8,128)(2,1)} %get-tuple-element.8.z_hbm) | copy-start | bytes 3538948
  127.6 25.3 %all-to-all-start.3 = ((bf16[128,4,1152]{2,1,0:T(4,128)(2,1)}), bf16[128,4,1152]{2,1,0:T(4,128)(2,1)S(1)}, u32[]{:S(2)}, u32[]{:S(2)}) async-start(bf16[128,4,1152]{2,1,0:T(4,128)(2,1)} %tri.3), calls=%async_computation.3 | async-start | bytes 2359296 | tf_op jit(solution)/shard_map/all_to_all | solution.py:362
